TPU v7x, 32 devices: a whole 2x2x4 slice. The times are simulated.
32 devices in a mesh: batch: 2 (over x), cols: 4 (over z), rows: 4 (over y, core).
Axes of the slice: x: 2, y: 2, z: 4, core: 2. Of those that a mesh axis runs over, the one named last changes fastest.
Arguments:
- frames: bfloat16 [8, 2, 96, 192, 16], P(None, 'batch', 'rows', 'cols'), parts along dimension 1
- h_init: float32 [2, 96, 192, 256], P('batch', 'rows', 'cols'), parts along dimension 0
- w_x: bfloat16 [3, 3, 16, 768], replicated
- w_hzr: bfloat16 [3, 3, 256, 512], replicated
- w_hn: bfloat16 [3, 3, 256, 256], replicated
- gate_bias: float32 [768], replicated
Outputs:
- output 1: bfloat16 [8, 2, 96, 192, 256], P(None, 'batch', 'rows', 'cols'), parts along dimension 1
- output 2: float32 [2, 96, 192, 256], P('batch', 'rows', 'cols'), parts along dimension 0
There are 2 independent parts. A program takes and returns all parts, laid end to end along the dimension named above; an argument that names none is the same for every part.
All inputs are finite; a program needn't handle non-finite values.
Results may differ from a plain program's by a relative error of at most 0.00325416.
Values are sent between devices in bfloat16 or wider.
A program may use at most 1 GiB of HBM per device.

v0:
```python
import jax
import jax.numpy as jnp
from jax import lax
from jax.sharding import PartitionSpec as P, NamedSharding


def with_halo(tile, width, n_rows, n_cols):
    tile_h = tile.shape[-3]
    tile_w = tile.shape[-2]
    down_pairs = [(dev_idx, dev_idx + 1) for dev_idx in range(n_rows - 1)]
    up_pairs = [(dev_idx + 1, dev_idx) for dev_idx in range(n_rows - 1)]
    from_above = lax.ppermute(tile[..., tile_h - width:, :, :], 'rows', down_pairs)
    from_below = lax.ppermute(tile[..., :width, :, :], 'rows', up_pairs)
    tall_tile = jnp.concatenate([from_above, tile, from_below], axis=-3)
    right_pairs = [(dev_idx, dev_idx + 1) for dev_idx in range(n_cols - 1)]
    left_pairs = [(dev_idx + 1, dev_idx) for dev_idx in range(n_cols - 1)]
    from_left = lax.ppermute(tall_tile[..., tile_w - width:, :], 'cols', right_pairs)
    from_right = lax.ppermute(tall_tile[..., :width, :], 'cols', left_pairs)
    return jnp.concatenate([from_left, tall_tile, from_right], axis=-2)


def im2col_conv(padded, w_mat):
    out_h = padded.shape[-3] - 2
    out_w = padded.shape[-2] - 2
    tap_list = [padded[..., row_off:row_off + out_h, col_off:col_off + out_w, :] for row_off in range(3) for col_off in range(3)]
    patches = jnp.concatenate(tap_list, axis=-1)
    return jnp.einsum('...k,kg->...g', patches, w_mat, preferred_element_type=jnp.float32)


def solution(mesh):
    n_rows = mesh.shape['rows']
    n_cols = mesh.shape['cols']
    frame_spec = P(None, 'batch', 'rows', 'cols', None)
    state_spec = P('batch', 'rows', 'cols', None)

    def local_fn(frames, h_init, w_x, w_hzr, w_hn, gate_bias):
        n_hidden = h_init.shape[-1]
        wx_mat = w_x.reshape(-1, w_x.shape[-1])
        whzr_mat = w_hzr.reshape(-1, w_hzr.shape[-1])
        whn_mat = w_hn.reshape(-1, w_hn.shape[-1])
        frames_pad = with_halo(frames, 1, n_rows, n_cols)

        def one_step(h_prev, frame_pad):
            gate_x = im2col_conv(frame_pad, wx_mat) + gate_bias
            h_pad = with_halo(h_prev.astype(jnp.bfloat16), 1, n_rows, n_cols)
            zr_gates = jax.nn.sigmoid(gate_x[..., :2 * n_hidden] + im2col_conv(h_pad, whzr_mat))
            update = zr_gates[..., :n_hidden]
            reset_pad = with_halo((zr_gates[..., n_hidden:] * h_prev).astype(jnp.bfloat16), 1, n_rows, n_cols)
            candidate = jnp.tanh(gate_x[..., 2 * n_hidden:] + im2col_conv(reset_pad, whn_mat))
            h_next = (1.0 - update) * candidate + update * h_prev
            return h_next, h_next.astype(jnp.bfloat16)

        h_last, h_seq = lax.scan(one_step, h_init, frames_pad)
        return h_seq, h_last

    return jax.shard_map(local_fn, mesh=mesh, in_specs=(frame_spec, state_spec, P(), P(), P(), P()), out_specs=(frame_spec, state_spec), check_vma=False)
```

profile of v0, /device:TPU:0, one launch (start us, length us, event | category | flops | bytes accessed | tf_op | source)
XLA Modules:
  0.0 432.0 jit_solution(18066665928258472757)
XLA Ops:
  27.2 403.8 %while.12 = (s32[]{:T(128)}, f32[1,24,48,256]{3,2,1,0:T(8,128)S(1)}, bf16[8,1,24,48,256]{4,3,2,1,0:T(8,128)(2,1)}, bf16[8,1,26,50,16]{3,4,2,1,0:T(8,128)(2,1)}, ...) while((s32[]{:T(128)}, ...), condition=%wide.region_1.2_spmd, body=%wide.region_0.1_spmd.sunk | while | flops 4353175552 | bytes 104953888 | solution.py:53
  41.5 4.5 %collective-permute-start.3 = (bf16[1,26,1,256]{3,2,1,0:T(2,128)(2,1)S(1)}, bf16[1,26,1,256]{3,2,1,0:T(2,128)(2,1)S(1)}, u32[]{:S(2)}, u32[]{:S(2)}) collective-permute-start(bf16[1,26,1,256]{3,2,1,0:T(2,128)(2,1)S(1)} %get-tuple-element.190), channel_id=1, source_target_pairs={{0,4},{4,8},{8,12},{1,5},{5,9},{9,13},{2,6},{6,10},{10,14},{3,7},{... | collective-permute-start | bytes 39944 | tf_op jit(solution)/shard_map/while/body/eval_jaxpr/ppermute | solution.py:17
  63.4 4.9 %collective-permute-start.7 = (bf16[1,26,1,256]{3,2,1,0:T(2,128)(2,1)S(1)}, bf16[1,26,1,256]{3,2,1,0:T(2,128)(2,1)S(1)}, u32[]{:S(2)}, u32[]{:S(2)}) collective-permute-start(bf16[1,26,1,256]{3,2,1,0:T(2,128)(2,1)S(1)} %get-tuple-element.196), channel_id=1, source_target_pairs={{0,4},{4,8},{8,12},{1,5},{5,9},{9,13},{2,6},{6,10},{10,14},{3,7},{... | collective-permute-start | bytes 39944 | tf_op jit(solution)/shard_map/while/body/eval_jaxpr/ppermute | solution.py:17
  90.0 4.8 %collective-permute-start.3 = (bf16[1,26,1,256]{3,2,1,0:T(2,128)(2,1)S(1)}, bf16[1,26,1,256]{3,2,1,0:T(2,128)(2,1)S(1)}, u32[]{:S(2)}, u32[]{:S(2)}) collective-permute-start(bf16[1,26,1,256]{3,2,1,0:T(2,128)(2,1)S(1)} %get-tuple-element.190), channel_id=1, source_target_pairs={{0,4},{4,8},{8,12},{1,5},{5,9},{9,13},{2,6},{6,10},{10,14},{3,7},{... | collective-permute-start | bytes 39944 | tf_op jit(solution)/shard_map/while/body/eval_jaxpr/ppermute | solution.py:17
  106.9 5.0 %collective-permute-start.5 = (bf16[1,1,48,256]{3,2,1,0:T(8,128)(2,1)S(1)}, bf16[1,1,48,256]{3,2,1,0:T(8,128)(2,1)S(1)}, u32[]{:S(2)}, u32[]{:S(2)}) collective-permute-start(bf16[1,1,48,256]{3,2,1,0:T(8,128)(2,1)S(1)} %get-tuple-element.194), channel_id=1, source_target_pairs={{0,1},{1,2},{2,3},{4,5},{5,6},{6,7},{8,9},{9,10},{10,11},{12,13},{... | collective-permute-start | bytes 73736 | tf_op jit(solution)/shard_map/while/body/eval_jaxpr/ppermute | solution.py:12
  114.1 4.5 %collective-permute-start.7 = (bf16[1,26,1,256]{3,2,1,0:T(2,128)(2,1)S(1)}, bf16[1,26,1,256]{3,2,1,0:T(2,128)(2,1)S(1)}, u32[]{:S(2)}, u32[]{:S(2)}) collective-permute-start(bf16[1,26,1,256]{3,2,1,0:T(2,128)(2,1)S(1)} %get-tuple-element.196), channel_id=1, source_target_pairs={{0,4},{4,8},{8,12},{1,5},{5,9},{9,13},{2,6},{6,10},{10,14},{3,7},{... | collective-permute-start | bytes 39944 | tf_op jit(solution)/shard_map/while/body/eval_jaxpr/ppermute | solution.py:17
  140.8 4.5 %collective-permute-start.3 = (bf16[1,26,1,256]{3,2,1,0:T(2,128)(2,1)S(1)}, bf16[1,26,1,256]{3,2,1,0:T(2,128)(2,1)S(1)}, u32[]{:S(2)}, u32[]{:S(2)}) collective-permute-start(bf16[1,26,1,256]{3,2,1,0:T(2,128)(2,1)S(1)} %get-tuple-element.190), channel_id=1, source_target_pairs={{0,4},{4,8},{8,12},{1,5},{5,9},{9,13},{2,6},{6,10},{10,14},{3,7},{... | collective-permute-start | bytes 39944 | tf_op jit(solution)/shard_map/while/body/eval_jaxpr/ppermute | solution.py:17
  157.4 5.2 %collective-permute-start.5 = (bf16[1,1,48,256]{3,2,1,0:T(8,128)(2,1)S(1)}, bf16[1,1,48,256]{3,2,1,0:T(8,128)(2,1)S(1)}, u32[]{:S(2)}, u32[]{:S(2)}) collective-permute-start(bf16[1,1,48,256]{3,2,1,0:T(8,128)(2,1)S(1)} %get-tuple-element.194), channel_id=1, source_target_pairs={{0,1},{1,2},{2,3},{4,5},{5,6},{6,7},{8,9},{9,10},{10,11},{12,13},{... | collective-permute-start | bytes 73736 | tf_op jit(solution)/shard_map/while/body/eval_jaxpr/ppermute | solution.py:12
  164.8 4.5 %collective-permute-start.7 = (bf16[1,26,1,256]{3,2,1,0:T(2,128)(2,1)S(1)}, bf16[1,26,1,256]{3,2,1,0:T(2,128)(2,1)S(1)}, u32[]{:S(2)}, u32[]{:S(2)}) collective-permute-start(bf16[1,26,1,256]{3,2,1,0:T(2,128)(2,1)S(1)} %get-tuple-element.196), channel_id=1, source_target_pairs={{0,4},{4,8},{8,12},{1,5},{5,9},{9,13},{2,6},{6,10},{10,14},{3,7},{... | collective-permute-start | bytes 39944 | tf_op jit(solution)/shard_map/while/body/eval_jaxpr/ppermute | solution.py:17
  191.5 4.5 %collective-permute-start.3 = (bf16[1,26,1,256]{3,2,1,0:T(2,128)(2,1)S(1)}, bf16[1,26,1,256]{3,2,1,0:T(2,128)(2,1)S(1)}, u32[]{:S(2)}, u32[]{:S(2)}) collective-permute-start(bf16[1,26,1,256]{3,2,1,0:T(2,128)(2,1)S(1)} %get-tuple-element.190), channel_id=1, source_target_pairs={{0,4},{4,8},{8,12},{1,5},{5,9},{9,13},{2,6},{6,10},{10,14},{3,7},{... | collective-permute-start | bytes 39944 | tf_op jit(solution)/shard_map/while/body/eval_jaxpr/ppermute | solution.py:17
  208.1 5.2 %collective-permute-start.5 = (bf16[1,1,48,256]{3,2,1,0:T(8,128)(2,1)S(1)}, bf16[1,1,48,256]{3,2,1,0:T(8,128)(2,1)S(1)}, u32[]{:S(2)}, u32[]{:S(2)}) collective-permute-start(bf16[1,1,48,256]{3,2,1,0:T(8,128)(2,1)S(1)} %get-tuple-element.194), channel_id=1, source_target_pairs={{0,1},{1,2},{2,3},{4,5},{5,6},{6,7},{8,9},{9,10},{10,11},{12,13},{... | collective-permute-start | bytes 73736 | tf_op jit(solution)/shard_map/while/body/eval_jaxpr/ppermute | solution.py:12
  215.5 4.5 %collective-permute-start.7 = (bf16[1,26,1,256]{3,2,1,0:T(2,128)(2,1)S(1)}, bf16[1,26,1,256]{3,2,1,0:T(2,128)(2,1)S(1)}, u32[]{:S(2)}, u32[]{:S(2)}) collective-permute-start(bf16[1,26,1,256]{3,2,1,0:T(2,128)(2,1)S(1)} %get-tuple-element.196), channel_id=1, source_target_pairs={{0,4},{4,8},{8,12},{1,5},{5,9},{9,13},{2,6},{6,10},{10,14},{3,7},{... | collective-permute-start | bytes 39944 | tf_op jit(solution)/shard_map/while/body/eval_jaxpr/ppermute | solution.py:17
  242.2 4.5 %collective-permute-start.3 = (bf16[1,26,1,256]{3,2,1,0:T(2,128)(2,1)S(1)}, bf16[1,26,1,256]{3,2,1,0:T(2,128)(2,1)S(1)}, u32[]{:S(2)}, u32[]{:S(2)}) collective-permute-start(bf16[1,26,1,256]{3,2,1,0:T(2,128)(2,1)S(1)} %get-tuple-element.190), channel_id=1, source_target_pairs={{0,4},{4,8},{8,12},{1,5},{5,9},{9,13},{2,6},{6,10},{10,14},{3,7},{... | collective-permute-start | bytes 39944 | tf_op jit(solution)/shard_map/while/body/eval_jaxpr/ppermute | solution.py:17
  258.8 5.2 %collective-permute-start.5 = (bf16[1,1,48,256]{3,2,1,0:T(8,128)(2,1)S(1)}, bf16[1,1,48,256]{3,2,1,0:T(8,128)(2,1)S(1)}, u32[]{:S(2)}, u32[]{:S(2)}) collective-permute-start(bf16[1,1,48,256]{3,2,1,0:T(8,128)(2,1)S(1)} %get-tuple-element.194), channel_id=1, source_target_pairs={{0,1},{1,2},{2,3},{4,5},{5,6},{6,7},{8,9},{9,10},{10,11},{12,13},{... | collective-permute-start | bytes 73736 | tf_op jit(solution)/shard_map/while/body/eval_jaxpr/ppermute | solution.py:12
  266.2 4.5 %collective-permute-start.7 = (bf16[1,26,1,256]{3,2,1,0:T(2,128)(2,1)S(1)}, bf16[1,26,1,256]{3,2,1,0:T(2,128)(2,1)S(1)}, u32[]{:S(2)}, u32[]{:S(2)}) collective-permute-start(bf16[1,26,1,256]{3,2,1,0:T(2,128)(2,1)S(1)} %get-tuple-element.196), channel_id=1, source_target_pairs={{0,4},{4,8},{8,12},{1,5},{5,9},{9,13},{2,6},{6,10},{10,14},{3,7},{... | collective-permute-start | bytes 39944 | tf_op jit(solution)/shard_map/while/body/eval_jaxpr/ppermute | solution.py:17
  292.9 4.5 %collective-permute-start.3 = (bf16[1,26,1,256]{3,2,1,0:T(2,128)(2,1)S(1)}, bf16[1,26,1,256]{3,2,1,0:T(2,128)(2,1)S(1)}, u32[]{:S(2)}, u32[]{:S(2)}) collective-permute-start(bf16[1,26,1,256]{3,2,1,0:T(2,128)(2,1)S(1)} %get-tuple-element.190), channel_id=1, source_target_pairs={{0,4},{4,8},{8,12},{1,5},{5,9},{9,13},{2,6},{6,10},{10,14},{3,7},{... | collective-permute-start | bytes 39944 | tf_op jit(solution)/shard_map/while/body/eval_jaxpr/ppermute | solution.py:17
  309.4 5.2 %collective-permute-start.5 = (bf16[1,1,48,256]{3,2,1,0:T(8,128)(2,1)S(1)}, bf16[1,1,48,256]{3,2,1,0:T(8,128)(2,1)S(1)}, u32[]{:S(2)}, u32[]{:S(2)}) collective-permute-start(bf16[1,1,48,256]{3,2,1,0:T(8,128)(2,1)S(1)} %get-tuple-element.194), channel_id=1, source_target_pairs={{0,1},{1,2},{2,3},{4,5},{5,6},{6,7},{8,9},{9,10},{10,11},{12,13},{... | collective-permute-start | bytes 73736 | tf_op jit(solution)/shard_map/while/body/eval_jaxpr/ppermute | solution.py:12
  316.9 4.5 %collective-permute-start.7 = (bf16[1,26,1,256]{3,2,1,0:T(2,128)(2,1)S(1)}, bf16[1,26,1,256]{3,2,1,0:T(2,128)(2,1)S(1)}, u32[]{:S(2)}, u32[]{:S(2)}) collective-permute-start(bf16[1,26,1,256]{3,2,1,0:T(2,128)(2,1)S(1)} %get-tuple-element.196), channel_id=1, source_target_pairs={{0,4},{4,8},{8,12},{1,5},{5,9},{9,13},{2,6},{6,10},{10,14},{3,7},{... | collective-permute-start | bytes 39944 | tf_op jit(solution)/shard_map/while/body/eval_jaxpr/ppermute | solution.py:17
  343.6 4.5 %collective-permute-start.3 = (bf16[1,26,1,256]{3,2,1,0:T(2,128)(2,1)S(1)}, bf16[1,26,1,256]{3,2,1,0:T(2,128)(2,1)S(1)}, u32[]{:S(2)}, u32[]{:S(2)}) collective-permute-start(bf16[1,26,1,256]{3,2,1,0:T(2,128)(2,1)S(1)} %get-tuple-element.190), channel_id=1, source_target_pairs={{0,4},{4,8},{8,12},{1,5},{5,9},{9,13},{2,6},{6,10},{10,14},{3,7},{... | collective-permute-start | bytes 39944 | tf_op jit(solution)/shard_map/while/body/eval_jaxpr/ppermute | solution.py:17
  360.1 5.2 %collective-permute-start.5 = (bf16[1,1,48,256]{3,2,1,0:T(8,128)(2,1)S(1)}, bf16[1,1,48,256]{3,2,1,0:T(8,128)(2,1)S(1)}, u32[]{:S(2)}, u32[]{:S(2)}) collective-permute-start(bf16[1,1,48,256]{3,2,1,0:T(8,128)(2,1)S(1)} %get-tuple-element.194), channel_id=1, source_target_pairs={{0,1},{1,2},{2,3},{4,5},{5,6},{6,7},{8,9},{9,10},{10,11},{12,13},{... | collective-permute-start | bytes 73736 | tf_op jit(solution)/shard_map/while/body/eval_jaxpr/ppermute | solution.py:12
  367.6 4.5 %collective-permute-start.7 = (bf16[1,26,1,256]{3,2,1,0:T(2,128)(2,1)S(1)}, bf16[1,26,1,256]{3,2,1,0:T(2,128)(2,1)S(1)}, u32[]{:S(2)}, u32[]{:S(2)}) collective-permute-start(bf16[1,26,1,256]{3,2,1,0:T(2,128)(2,1)S(1)} %get-tuple-element.196), channel_id=1, source_target_pairs={{0,4},{4,8},{8,12},{1,5},{5,9},{9,13},{2,6},{6,10},{10,14},{3,7},{... | collective-permute-start | bytes 39944 | tf_op jit(solution)/shard_map/while/body/eval_jaxpr/ppermute | solution.py:17
  394.2 4.5 %collective-permute-start.3 = (bf16[1,26,1,256]{3,2,1,0:T(2,128)(2,1)S(1)}, bf16[1,26,1,256]{3,2,1,0:T(2,128)(2,1)S(1)}, u32[]{:S(2)}, u32[]{:S(2)}) collective-permute-start(bf16[1,26,1,256]{3,2,1,0:T(2,128)(2,1)S(1)} %get-tuple-element.190), channel_id=1, source_target_pairs={{0,4},{4,8},{8,12},{1,5},{5,9},{9,13},{2,6},{6,10},{10,14},{3,7},{... | collective-permute-start | bytes 39944 | tf_op jit(solution)/shard_map/while/body/eval_jaxpr/ppermute | solution.py:17
  410.8 5.2 %collective-permute-start.5 = (bf16[1,1,48,256]{3,2,1,0:T(8,128)(2,1)S(1)}, bf16[1,1,48,256]{3,2,1,0:T(8,128)(2,1)S(1)}, u32[]{:S(2)}, u32[]{:S(2)}) collective-permute-start(bf16[1,1,48,256]{3,2,1,0:T(8,128)(2,1)S(1)} %get-tuple-element.194), channel_id=1, source_target_pairs={{0,1},{1,2},{2,3},{4,5},{5,6},{6,7},{8,9},{9,10},{10,11},{12,13},{... | collective-permute-start | bytes 73736 | tf_op jit(solution)/shard_map/while/body/eval_jaxpr/ppermute | solution.py:12
  418.3 4.5 %collective-permute-start.7 = (bf16[1,26,1,256]{3,2,1,0:T(2,128)(2,1)S(1)}, bf16[1,26,1,256]{3,2,1,0:T(2,128)(2,1)S(1)}, u32[]{:S(2)}, u32[]{:S(2)}) collective-permute-start(bf16[1,26,1,256]{3,2,1,0:T(2,128)(2,1)S(1)} %get-tuple-element.196), channel_id=1, source_target_pairs={{0,4},{4,8},{8,12},{1,5},{5,9},{9,13},{2,6},{6,10},{10,14},{3,7},{... | collective-permute-start | bytes 39944 | tf_op jit(solution)/shard_map/while/body/eval_jaxpr/ppermute | solution.py:17
  (464 shorter events, 319.1 us)
Async XLA Ops:
  27.9 11.5 %collective-permute-start = (bf16[1,1,48,256]{3,2,1,0:T(8,128)(2,1)}, bf16[1,1,48,256]{3,2,1,0:T(8,128)(2,1)}, u32[]{:S(2)}, u32[]{:S(2)}) collective-permute-start(bf16[1,1,48,256]{3,2,1,0:T(8,128)(2,1)} %get-tuple-element.187), channel_id=1, source_target_pairs={{1,0},{2,1},{3,2},{5,4},{6,5},{7,6},{9,8},{10,9},{11,10},{13,12},{... | collective-permute-start | bytes 73736 | tf_op jit(solution)/shard_map/while/body/eval_jaxpr/ppermute | solution.py:13
  29.2 10.2 %collective-permute-start.1 = (bf16[1,1,48,256]{3,2,1,0:T(8,128)(2,1)}, bf16[1,1,48,256]{3,2,1,0:T(8,128)(2,1)}, u32[]{:S(2)}, u32[]{:S(2)}) collective-permute-start(bf16[1,1,48,256]{3,2,1,0:T(8,128)(2,1)} %get-tuple-element.188), channel_id=1, source_target_pairs={{0,1},{1,2},{2,3},{4,5},{5,6},{6,7},{8,9},{9,10},{10,11},{12,13},{... | collective-permute-start | bytes 73736 | tf_op jit(solution)/shard_map/while/body/eval_jaxpr/ppermute | solution.py:12
  40.2 7.4 %collective-permute-start.2 = (bf16[1,26,1,256]{3,2,1,0:T(2,128)(2,1)S(1)}, bf16[1,26,1,256]{3,2,1,0:T(2,128)(2,1)S(1)}, u32[]{:S(2)}, u32[]{:S(2)}) collective-permute-start(bf16[1,26,1,256]{3,2,1,0:T(2,128)(2,1)S(1)} %get-tuple-element.189), channel_id=1, source_target_pairs={{4,0},{8,4},{12,8},{5,1},{9,5},{13,9},{6,2},{10,6},{14,10},{7,3},{... | collective-permute-start | bytes 39944 | tf_op jit(solution)/shard_map/while/body/eval_jaxpr/ppermute | solution.py:18
  77.2 10.8 %collective-permute-start = (bf16[1,1,48,256]{3,2,1,0:T(8,128)(2,1)}, bf16[1,1,48,256]{3,2,1,0:T(8,128)(2,1)}, u32[]{:S(2)}, u32[]{:S(2)}) collective-permute-start(bf16[1,1,48,256]{3,2,1,0:T(8,128)(2,1)} %get-tuple-element.187), channel_id=1, source_target_pairs={{1,0},{2,1},{3,2},{5,4},{6,5},{7,6},{9,8},{10,9},{11,10},{13,12},{... | collective-permute-start | bytes 73736 | tf_op jit(solution)/shard_map/while/body/eval_jaxpr/ppermute | solution.py:13
  78.4 9.5 %collective-permute-start.1 = (bf16[1,1,48,256]{3,2,1,0:T(8,128)(2,1)}, bf16[1,1,48,256]{3,2,1,0:T(8,128)(2,1)}, u32[]{:S(2)}, u32[]{:S(2)}) collective-permute-start(bf16[1,1,48,256]{3,2,1,0:T(8,128)(2,1)} %get-tuple-element.188), channel_id=1, source_target_pairs={{0,1},{1,2},{2,3},{4,5},{5,6},{6,7},{8,9},{9,10},{10,11},{12,13},{... | collective-permute-start | bytes 73736 | tf_op jit(solution)/shard_map/while/body/eval_jaxpr/ppermute | solution.py:12
  88.7 7.7 %collective-permute-start.2 = (bf16[1,26,1,256]{3,2,1,0:T(2,128)(2,1)S(1)}, bf16[1,26,1,256]{3,2,1,0:T(2,128)(2,1)S(1)}, u32[]{:S(2)}, u32[]{:S(2)}) collective-permute-start(bf16[1,26,1,256]{3,2,1,0:T(2,128)(2,1)S(1)} %get-tuple-element.189), channel_id=1, source_target_pairs={{4,0},{8,4},{12,8},{5,1},{9,5},{13,9},{6,2},{10,6},{14,10},{7,3},{... | collective-permute-start | bytes 39944 | tf_op jit(solution)/shard_map/while/body/eval_jaxpr/ppermute | solution.py:18
  127.5 11.2 %collective-permute-start = (bf16[1,1,48,256]{3,2,1,0:T(8,128)(2,1)}, bf16[1,1,48,256]{3,2,1,0:T(8,128)(2,1)}, u32[]{:S(2)}, u32[]{:S(2)}) collective-permute-start(bf16[1,1,48,256]{3,2,1,0:T(8,128)(2,1)} %get-tuple-element.187), channel_id=1, source_target_pairs={{1,0},{2,1},{3,2},{5,4},{6,5},{7,6},{9,8},{10,9},{11,10},{13,12},{... | collective-permute-start | bytes 73736 | tf_op jit(solution)/shard_map/while/body/eval_jaxpr/ppermute | solution.py:13
  128.8 9.9 %collective-permute-start.1 = (bf16[1,1,48,256]{3,2,1,0:T(8,128)(2,1)}, bf16[1,1,48,256]{3,2,1,0:T(8,128)(2,1)}, u32[]{:S(2)}, u32[]{:S(2)}) collective-permute-start(bf16[1,1,48,256]{3,2,1,0:T(8,128)(2,1)} %get-tuple-element.188), channel_id=1, source_target_pairs={{0,1},{1,2},{2,3},{4,5},{5,6},{6,7},{8,9},{9,10},{10,11},{12,13},{... | collective-permute-start | bytes 73736 | tf_op jit(solution)/shard_map/while/body/eval_jaxpr/ppermute | solution.py:12
  139.5 7.4 %collective-permute-start.2 = (bf16[1,26,1,256]{3,2,1,0:T(2,128)(2,1)S(1)}, bf16[1,26,1,256]{3,2,1,0:T(2,128)(2,1)S(1)}, u32[]{:S(2)}, u32[]{:S(2)}) collective-permute-start(bf16[1,26,1,256]{3,2,1,0:T(2,128)(2,1)S(1)} %get-tuple-element.189), channel_id=1, source_target_pairs={{4,0},{8,4},{12,8},{5,1},{9,5},{13,9},{6,2},{10,6},{14,10},{7,3},{... | collective-permute-start | bytes 39944 | tf_op jit(solution)/shard_map/while/body/eval_jaxpr/ppermute | solution.py:18
  178.2 11.2 %collective-permute-start = (bf16[1,1,48,256]{3,2,1,0:T(8,128)(2,1)}, bf16[1,1,48,256]{3,2,1,0:T(8,128)(2,1)}, u32[]{:S(2)}, u32[]{:S(2)}) collective-permute-start(bf16[1,1,48,256]{3,2,1,0:T(8,128)(2,1)} %get-tuple-element.187), channel_id=1, source_target_pairs={{1,0},{2,1},{3,2},{5,4},{6,5},{7,6},{9,8},{10,9},{11,10},{13,12},{... | collective-permute-start | bytes 73736 | tf_op jit(solution)/shard_map/while/body/eval_jaxpr/ppermute | solution.py:13
  179.5 9.9 %collective-permute-start.1 = (bf16[1,1,48,256]{3,2,1,0:T(8,128)(2,1)}, bf16[1,1,48,256]{3,2,1,0:T(8,128)(2,1)}, u32[]{:S(2)}, u32[]{:S(2)}) collective-permute-start(bf16[1,1,48,256]{3,2,1,0:T(8,128)(2,1)} %get-tuple-element.188), channel_id=1, source_target_pairs={{0,1},{1,2},{2,3},{4,5},{5,6},{6,7},{8,9},{9,10},{10,11},{12,13},{... | collective-permute-start | bytes 73736 | tf_op jit(solution)/shard_map/while/body/eval_jaxpr/ppermute | solution.py:12
  190.2 7.4 %collective-permute-start.2 = (bf16[1,26,1,256]{3,2,1,0:T(2,128)(2,1)S(1)}, bf16[1,26,1,256]{3,2,1,0:T(2,128)(2,1)S(1)}, u32[]{:S(2)}, u32[]{:S(2)}) collective-permute-start(bf16[1,26,1,256]{3,2,1,0:T(2,128)(2,1)S(1)} %get-tuple-element.189), channel_id=1, source_target_pairs={{4,0},{8,4},{12,8},{5,1},{9,5},{13,9},{6,2},{10,6},{14,10},{7,3},{... | collective-permute-start | bytes 39944 | tf_op jit(solution)/shard_map/while/body/eval_jaxpr/ppermute | solution.py:18
  228.9 11.2 %collective-permute-start = (bf16[1,1,48,256]{3,2,1,0:T(8,128)(2,1)}, bf16[1,1,48,256]{3,2,1,0:T(8,128)(2,1)}, u32[]{:S(2)}, u32[]{:S(2)}) collective-permute-start(bf16[1,1,48,256]{3,2,1,0:T(8,128)(2,1)} %get-tuple-element.187), channel_id=1, source_target_pairs={{1,0},{2,1},{3,2},{5,4},{6,5},{7,6},{9,8},{10,9},{11,10},{13,12},{... | collective-permute-start | bytes 73736 | tf_op jit(solution)/shard_map/while/body/eval_jaxpr/ppermute | solution.py:13
  230.2 9.9 %collective-permute-start.1 = (bf16[1,1,48,256]{3,2,1,0:T(8,128)(2,1)}, bf16[1,1,48,256]{3,2,1,0:T(8,128)(2,1)}, u32[]{:S(2)}, u32[]{:S(2)}) collective-permute-start(bf16[1,1,48,256]{3,2,1,0:T(8,128)(2,1)} %get-tuple-element.188), channel_id=1, source_target_pairs={{0,1},{1,2},{2,3},{4,5},{5,6},{6,7},{8,9},{9,10},{10,11},{12,13},{... | collective-permute-start | bytes 73736 | tf_op jit(solution)/shard_map/while/body/eval_jaxpr/ppermute | solution.py:12
  240.9 7.4 %collective-permute-start.2 = (bf16[1,26,1,256]{3,2,1,0:T(2,128)(2,1)S(1)}, bf16[1,26,1,256]{3,2,1,0:T(2,128)(2,1)S(1)}, u32[]{:S(2)}, u32[]{:S(2)}) collective-permute-start(bf16[1,26,1,256]{3,2,1,0:T(2,128)(2,1)S(1)} %get-tuple-element.189), channel_id=1, source_target_pairs={{4,0},{8,4},{12,8},{5,1},{9,5},{13,9},{6,2},{10,6},{14,10},{7,3},{... | collective-permute-start | bytes 39944 | tf_op jit(solution)/shard_map/while/body/eval_jaxpr/ppermute | solution.py:18
  279.6 11.2 %collective-permute-start = (bf16[1,1,48,256]{3,2,1,0:T(8,128)(2,1)}, bf16[1,1,48,256]{3,2,1,0:T(8,128)(2,1)}, u32[]{:S(2)}, u32[]{:S(2)}) collective-permute-start(bf16[1,1,48,256]{3,2,1,0:T(8,128)(2,1)} %get-tuple-element.187), channel_id=1, source_target_pairs={{1,0},{2,1},{3,2},{5,4},{6,5},{7,6},{9,8},{10,9},{11,10},{13,12},{... | collective-permute-start | bytes 73736 | tf_op jit(solution)/shard_map/while/body/eval_jaxpr/ppermute | solution.py:13
  280.9 9.9 %collective-permute-start.1 = (bf16[1,1,48,256]{3,2,1,0:T(8,128)(2,1)}, bf16[1,1,48,256]{3,2,1,0:T(8,128)(2,1)}, u32[]{:S(2)}, u32[]{:S(2)}) collective-permute-start(bf16[1,1,48,256]{3,2,1,0:T(8,128)(2,1)} %get-tuple-element.188), channel_id=1, source_target_pairs={{0,1},{1,2},{2,3},{4,5},{5,6},{6,7},{8,9},{9,10},{10,11},{12,13},{... | collective-permute-start | bytes 73736 | tf_op jit(solution)/shard_map/while/body/eval_jaxpr/ppermute | solution.py:12
  291.6 7.4 %collective-permute-start.2 = (bf16[1,26,1,256]{3,2,1,0:T(2,128)(2,1)S(1)}, bf16[1,26,1,256]{3,2,1,0:T(2,128)(2,1)S(1)}, u32[]{:S(2)}, u32[]{:S(2)}) collective-permute-start(bf16[1,26,1,256]{3,2,1,0:T(2,128)(2,1)S(1)} %get-tuple-element.189), channel_id=1, source_target_pairs={{4,0},{8,4},{12,8},{5,1},{9,5},{13,9},{6,2},{10,6},{14,10},{7,3},{... | collective-permute-start | bytes 39944 | tf_op jit(solution)/shard_map/while/body/eval_jaxpr/ppermute | solution.py:18
  330.3 11.2 %collective-permute-start = (bf16[1,1,48,256]{3,2,1,0:T(8,128)(2,1)}, bf16[1,1,48,256]{3,2,1,0:T(8,128)(2,1)}, u32[]{:S(2)}, u32[]{:S(2)}) collective-permute-start(bf16[1,1,48,256]{3,2,1,0:T(8,128)(2,1)} %get-tuple-element.187), channel_id=1, source_target_pairs={{1,0},{2,1},{3,2},{5,4},{6,5},{7,6},{9,8},{10,9},{11,10},{13,12},{... | collective-permute-start | bytes 73736 | tf_op jit(solution)/shard_map/while/body/eval_jaxpr/ppermute | solution.py:13
  331.6 9.9 %collective-permute-start.1 = (bf16[1,1,48,256]{3,2,1,0:T(8,128)(2,1)}, bf16[1,1,48,256]{3,2,1,0:T(8,128)(2,1)}, u32[]{:S(2)}, u32[]{:S(2)}) collective-permute-start(bf16[1,1,48,256]{3,2,1,0:T(8,128)(2,1)} %get-tuple-element.188), channel_id=1, source_target_pairs={{0,1},{1,2},{2,3},{4,5},{5,6},{6,7},{8,9},{9,10},{10,11},{12,13},{... | collective-permute-start | bytes 73736 | tf_op jit(solution)/shard_map/while/body/eval_jaxpr/ppermute | solution.py:12
  342.3 7.4 %collective-permute-start.2 = (bf16[1,26,1,256]{3,2,1,0:T(2,128)(2,1)S(1)}, bf16[1,26,1,256]{3,2,1,0:T(2,128)(2,1)S(1)}, u32[]{:S(2)}, u32[]{:S(2)}) collective-permute-start(bf16[1,26,1,256]{3,2,1,0:T(2,128)(2,1)S(1)} %get-tuple-element.189), channel_id=1, source_target_pairs={{4,0},{8,4},{12,8},{5,1},{9,5},{13,9},{6,2},{10,6},{14,10},{7,3},{... | collective-permute-start | bytes 39944 | tf_op jit(solution)/shard_map/while/body/eval_jaxpr/ppermute | solution.py:18
  381.0 11.2 %collective-permute-start = (bf16[1,1,48,256]{3,2,1,0:T(8,128)(2,1)}, bf16[1,1,48,256]{3,2,1,0:T(8,128)(2,1)}, u32[]{:S(2)}, u32[]{:S(2)}) collective-permute-start(bf16[1,1,48,256]{3,2,1,0:T(8,128)(2,1)} %get-tuple-element.187), channel_id=1, source_target_pairs={{1,0},{2,1},{3,2},{5,4},{6,5},{7,6},{9,8},{10,9},{11,10},{13,12},{... | collective-permute-start | bytes 73736 | tf_op jit(solution)/shard_map/while/body/eval_jaxpr/ppermute | solution.py:13
  382.3 9.9 %collective-permute-start.1 = (bf16[1,1,48,256]{3,2,1,0:T(8,128)(2,1)}, bf16[1,1,48,256]{3,2,1,0:T(8,128)(2,1)}, u32[]{:S(2)}, u32[]{:S(2)}) collective-permute-start(bf16[1,1,48,256]{3,2,1,0:T(8,128)(2,1)} %get-tuple-element.188), channel_id=1, source_target_pairs={{0,1},{1,2},{2,3},{4,5},{5,6},{6,7},{8,9},{9,10},{10,11},{12,13},{... | collective-permute-start | bytes 73736 | tf_op jit(solution)/shard_map/while/body/eval_jaxpr/ppermute | solution.py:12
  392.9 7.4 %collective-permute-start.2 = (bf16[1,26,1,256]{3,2,1,0:T(2,128)(2,1)S(1)}, bf16[1,26,1,256]{3,2,1,0:T(2,128)(2,1)S(1)}, u32[]{:S(2)}, u32[]{:S(2)}) collective-permute-start(bf16[1,26,1,256]{3,2,1,0:T(2,128)(2,1)S(1)} %get-tuple-element.189), channel_id=1, source_target_pairs={{4,0},{8,4},{12,8},{5,1},{9,5},{13,9},{6,2},{10,6},{14,10},{7,3},{... | collective-permute-start | bytes 39944 | tf_op jit(solution)/shard_map/while/body/eval_jaxpr/ppermute | solution.py:18
  (82 other events, 358.2 us)
where the time goes:
time: 441 us; the launch traced here: 432 us
  starting transfers between devices  195 us (44%)
  local copies, waits for them, and re-layouts  96.1 us (22%)
  matrix products  71.3 us (16%)
  other arithmetic  41.8 us (9%)
  waiting for transfers between devices  24.9 us (6%)
    ppermute x17, starting transfers between devices, with_halo(): lax.ppermute(tall_tile[..., tile_w - width:, :], 'cols', right_pairs)  76.8 us
    ppermute x17, starting transfers between devices, with_halo(): lax.ppermute(tile[..., tile_h - width:, :, :], 'rows', down_pairs)  73.9 us
    dot_general x24, matrix products, im2col_conv(): jnp.einsum('...k,kg->...g', patches, w_mat, preferred_element_type=jnp.fl...  71.3 us
    while x152, local copies, waits for them, and re-layouts  31.5 us
    concatenate x24, local copies, waits for them, and re-layouts, im2col_conv(): patches = jnp.concatenate(tap_list, axis=-1)  28.2 us
    ppermute x17, starting transfers between devices, with_halo(): from_right = lax.ppermute(tall_tile[..., :width, :], 'cols', left_pairs)  22.1 us
    ppermute x17, starting transfers between devices, with_halo(): from_below = lax.ppermute(tile[..., :width, :, :], 'rows', up_pairs)  21.9 us
    concatenate x17, other arithmetic, with_halo(): return jnp.concatenate([from_left, tall_tile, from_right], axis=-2)  18.3 us
  transfers between devices with their start and end apart: 68, of which 18 were waited for; matrix products, arithmetic and copies ran while one was open for 14% of the time, Pallas kernels for 0%

commit v1 on v0

v1 whole, which is shorter than its diff:
```python
import jax
import jax.numpy as jnp
from jax import lax
from jax.experimental import pallas as pl
from jax.experimental.pallas import tpu as pltpu
from jax.sharding import PartitionSpec as P

BF16 = jnp.bfloat16
F32 = jnp.float32
MESH = pl.DeviceIdType.MESH
LANES = 128
COL_HALO = 16
CHUNKS = (6, 6, 6, 6)
NAMES = ("batch", "cols", "rows")


def sigmoid(v):
    return 0.5 * jnp.tanh(0.5 * v) + 0.5


def kernel_body(n_cols, n_rows, dims, frames, h_init, w_x, w_hzr, w_hn, bias, h_seq, h_last,
                wzr, wn, wx, bv, fv, fp, hb, rb, xp, xe, af, h32, zb, hf, hl, cs, cr, kr, cb,
                load_sem, fsend, frecv, csend, crecv, ksend, krecv, vsend, vrecv, osem, lsem):
    steps, tile_h, tile_w, cin, ch = dims
    batch = lax.axis_index("batch")
    col = lax.axis_index("cols")
    row = lax.axis_index("rows")
    flip = lax.rem(row, 2)
    first_row = row - 1 + 2 * flip
    last_row = row + 1 - 2 * flip
    has_first = jnp.logical_and(first_row >= 0, first_row < n_rows)
    has_last = jnp.logical_and(last_row >= 0, last_row < n_rows)
    has_left = col > 0
    has_right = col < n_cols - 1
    both = jnp.logical_and
    left_dev = (batch, col - 1, row)
    right_dev = (batch, col + 1, row)
    first_dev = (batch, col, first_row)
    last_dev = (batch, col, last_row)
    corner_ok = (both(has_first, has_left), both(has_first, has_right), both(has_last, has_left), both(has_last, has_right))
    corner_dev = ((batch, col - 1, first_row), (batch, col + 1, first_row), (batch, col - 1, last_row), (batch, col + 1, last_row))
    around = ((has_left, left_dev), (has_right, right_dev), (has_first, first_dev), (has_last, last_dev)) + tuple(zip(corner_ok, corner_dev))

    def phys(i):
        return i + flip * (tile_h - 1 - 2 * i)

    n_chunks = len(CHUNKS)
    starts = [sum(CHUNKS[:k]) for k in range(n_chunks)]
    n_ranges = [(starts[k], CHUNKS[k]) for k in range(n_chunks)]
    r_ranges = []
    for k in range(n_chunks):
        lo = -1 if k == 0 else starts[k] + 1
        hi = tile_h + 1 if k == n_chunks - 1 else starts[k] + CHUNKS[k] + 1
        r_ranges.append((lo, hi - lo))

    def remote(src, dst, s_sem, r_sem, dev):
        return pltpu.make_async_remote_copy(src_ref=src, dst_ref=dst, send_sem=s_sem, recv_sem=r_sem, device_id=dev, device_id_type=MESH)

    loads = []
    for i in range(tile_h):
        loads.append(pltpu.make_async_copy(h_init.at[0, phys(i)], h32.at[i], load_sem.at[0, i]))
    frame_loads = [pltpu.make_async_copy(frames.at[:, 0, phys(i)], fv.at[i], load_sem.at[1, i]) for i in range(tile_h)]
    weight_loads = []
    for a in range(3):
        la = a + flip * (2 - 2 * a)
        weight_loads.append(pltpu.make_async_copy(w_hzr.at[a], wzr.at[la], load_sem.at[2, a]))
        weight_loads.append(pltpu.make_async_copy(w_hn.at[a], wn.at[la], load_sem.at[2, 3 + a]))
        for c in range(3):
            dst = wx.at[pl.ds(pl.multiple_of(64 * c + cin * la, cin), cin)]
            weight_loads.append(pltpu.make_async_copy(w_x.at[a, c], dst, load_sem.at[2, 6 + 3 * a + c]))
    weight_loads.append(pltpu.make_async_copy(bias, bv, load_sem.at[2, 15]))
    for copy in frame_loads + loads + weight_loads:
        copy.start()

    hf[...] = jnp.zeros_like(hf)
    hl[...] = jnp.zeros_like(hl)
    cr[...] = jnp.zeros_like(cr)
    kr[...] = jnp.zeros_like(kr)
    cb[...] = jnp.zeros_like(cb)
    cs[...] = jnp.zeros_like(cs)
    fp[...] = jnp.zeros_like(fp)
    for lo, hi in ((48, 64), (112, 128), (176, 256)):
        wx[lo:hi] = jnp.zeros((hi - lo, 3 * ch), BF16)

    barrier = pltpu.get_barrier_semaphore()
    count = 0
    for ok, dev in around:
        count = count + ok.astype(jnp.int32)

        @pl.when(ok)
        def _(dev=dev):
            pl.semaphore_signal(barrier, inc=1, device_id=dev, device_id_type=MESH)
    pl.semaphore_wait(barrier, count)

    lane = lax.broadcasted_iota(jnp.int32, (1, LANES), 1)

    for copy in frame_loads:
        copy.wait()
    own_c = pl.ds(COL_HALO, tile_w)
    for i in range(tile_h):
        fp[i + 2, own_c] = fv[i].reshape(steps * cin, tile_w).astype(F32).T.astype(BF16)

    lo_c = pl.ds(0, COL_HALO)
    hi_c = pl.ds(COL_HALO + tile_w, COL_HALO)
    own_lo = pl.ds(COL_HALO, COL_HALO)
    own_hi = pl.ds(tile_w, COL_HALO)
    f_copies = []
    own_r = pl.ds(2, tile_h)
    f_copies.append((has_left, fp.at[own_r, own_lo], fp.at[own_r, hi_c], left_dev))
    f_copies.append((has_right, fp.at[own_r, own_hi], fp.at[own_r, lo_c], right_dev))
    for ok, okl, okr, dev, cdl, cdr, rows in (
            (has_first, corner_ok[0], corner_ok[1], first_dev, corner_dev[0], corner_dev[1], ((2, 1), (3, 0))),
            (has_last, corner_ok[2], corner_ok[3], last_dev, corner_dev[2], corner_dev[3], ((tile_h + 1, tile_h + 2), (tile_h, tile_h + 3)))):
        for src, dst in rows:
            f_copies.append((ok, fp.at[src, own_c], fp.at[dst, own_c], dev))
            f_copies.append((okl, fp.at[src, own_lo], fp.at[dst, hi_c], cdl))
            f_copies.append((okr, fp.at[src, own_hi], fp.at[dst, lo_c], cdr))
    f_recv_index = [1, 0]
    for g in range(4):
        f_recv_index += [2 + 3 * g, 4 + 3 * g, 3 + 3 * g]
    f_descs = [(ok, remote(s, d, fsend.at[m], frecv.at[f_recv_index[m]], dev)) for m, (ok, s, d, dev) in enumerate(f_copies)]
    for ok, copy in f_descs:
        @pl.when(ok)
        def _(copy=copy):
            copy.start()

    def col_sends(k, slot):
        out = [(has_left, remote(cs.at[k, pl.ds(0, 2)], cr.at[slot, 1, k], csend.at[0, k], crecv.at[slot, 1, k], left_dev)),
               (has_right, remote(cs.at[k, pl.ds(2, 2)], cr.at[slot, 0, k], csend.at[1, k], crecv.at[slot, 0, k], right_dev))]
        if k == 0:
            out.append((has_first, remote(h32.at[pl.ds(0, 2)], hf.at[slot], vsend.at[0], vrecv.at[slot, 0], first_dev)))
            out.append((corner_ok[0], remote(cs.at[k, pl.ds(0, 2)], kr.at[slot, 1], ksend.at[0], krecv.at[slot, 1], corner_dev[0])))
            out.append((corner_ok[1], remote(cs.at[k, pl.ds(2, 2)], kr.at[slot, 0], ksend.at[1], krecv.at[slot, 0], corner_dev[1])))
        if k == n_chunks - 1:
            out.append((has_last, remote(h32.at[pl.ds(tile_h - 2, 2)], hl.at[slot], vsend.at[1], vrecv.at[slot, 1], last_dev)))
            out.append((corner_ok[2], remote(cs.at[k, pl.ds(0, 2)], kr.at[slot, 3], ksend.at[2], krecv.at[slot, 3], corner_dev[2])))
            out.append((corner_ok[3], remote(cs.at[k, pl.ds(2, 2)], kr.at[slot, 2], ksend.at[3], krecv.at[slot, 2], corner_dev[3])))
        return out

    def start_sends(k, slot, more):
        for ok, copy in col_sends(k, slot):
            @pl.when(both(ok, more))
            def _(copy=copy):
                copy.start()

    def wait_sends(k, slot):
        for ok, copy in col_sends(k, slot):
            @pl.when(ok)
            def _(copy=copy):
                copy.wait_send()

    def wait_if(ok, dst, sem, src):
        @pl.when(ok)
        def _():
            remote(src, dst, csend.at[0, 0], sem, right_dev).wait_recv()

    sub48 = lax.broadcasted_iota(jnp.int32, (tile_w, ch), 0)
    sub16 = lax.broadcasted_iota(jnp.int32, (16, ch), 0)

    def row_of(colbuf, i):
        return cb[colbuf, pl.ds(i + 8, 1), :]

    def publish(slot, i, v, k):
        hb[slot, 1, i + 2] = v.astype(BF16)
        hb[slot, 0, i + 2] = pltpu.roll(v, 1, 0).astype(BF16)
        hb[slot, 2, i + 2] = pltpu.roll(v, tile_w - 1, 0).astype(BF16)
        j = i - starts[k]
        for q, x in enumerate((0, 1, tile_w - 2, tile_w - 1)):
            cs[k, q, pl.ds(j, 1), :] = v[x:x + 1]
        cb[2, pl.ds(i + 8, 1), :] = v[0:1]
        cb[3, pl.ds(i + 8, 1), :] = v[tile_w - 1:tile_w]

    def arrive_cols(slot, k):
        wait_if(has_left, cr.at[slot, 0, k], crecv.at[slot, 0, k], cs.at[k, pl.ds(0, 2)])
        wait_if(has_right, cr.at[slot, 1, k], crecv.at[slot, 1, k], cs.at[k, pl.ds(0, 2)])
        i0, n = n_ranges[k]
        for side in range(2):
            for m in range(2):
                cb[4 * side + m, pl.ds(i0 + 8, n), :] = cr[slot, side, k, m, 0:n, :]
        for i in range(i0, i0 + n):
            old = hb[slot, 0, i + 2, 0:16].astype(F32)
            hb[slot, 0, i + 2, 0:16] = jnp.where(sub16 == 0, row_of(1, i), old).astype(BF16)
            old = hb[slot, 2, i + 2, tile_w - 16:tile_w].astype(F32)
            hb[slot, 2, i + 2, tile_w - 16:tile_w] = jnp.where(sub16 == 15, row_of(4, i), old).astype(BF16)

    def arrive_rows(slot, last):
        src, ok = (hl, has_last) if last else (hf, has_first)
        wait_if(ok, src.at[slot], vrecv.at[slot, last], h32.at[pl.ds(0, 2)])
        for m in range(2):
            q = 2 * last + m
            wait_if(corner_ok[q], kr.at[slot, q], krecv.at[slot, q], cs.at[0, pl.ds(0, 2)])
        for depth in range(2):
            i = tile_h + depth if last else -1 - depth
            m = 1 - depth if last else depth
            j = CHUNKS[-1] - 1 - depth if last else depth
            for x in range(2):
                cb[x, pl.ds(i + 8, 1), :] = kr[slot, 2 * last, x, j:j + 1, :]
                cb[4 + x, pl.ds(i + 8, 1), :] = kr[slot, 2 * last + 1, x, j:j + 1, :]
            v = src[slot, m]
            cb[2, pl.ds(i + 8, 1), :] = v[0:1]
            cb[3, pl.ds(i + 8, 1), :] = v[tile_w - 1:tile_w]
            hb[slot, 1, i + 2] = v.astype(BF16)
            hb[slot, 0, i + 2] = jnp.where(sub48 == 0, row_of(1, i), pltpu.roll(v, 1, 0)).astype(BF16)
            hb[slot, 2, i + 2] = jnp.where(sub48 == tile_w - 1, row_of(4, i), pltpu.roll(v, tile_w - 1, 0)).astype(BF16)

    wide = tile_w + 2 * COL_HALO

    def build_x(t, slot, k):
        i0, n = r_ranges[k]
        for j in range(n):
            parts = [pltpu.roll(fp[i0 + j + a + 1].astype(F32), lax.rem(cin * a - cin * t + cin * steps, cin * steps), 1) for a in range(3)]
            af[pl.ds(j * wide, wide)] = jnp.where(lane < cin, parts[0], jnp.where(lane < 2 * cin, parts[1], parts[2]))
        for j in range(n):
            base = j * wide + COL_HALO
            left = af[pl.ds(base - 1, tile_w)]
            mid = pltpu.roll(af[pl.ds(base, tile_w)], 64, 1)
            xp[slot, i0 + j + 1, :, 0:LANES] = jnp.where(lane < 64, left, mid).astype(BF16)
            xp[slot, i0 + j + 1, :, LANES:2 * LANES] = af[pl.ds(base + 1, tile_w)].astype(BF16)
        lo_half, hi_half = [], []
        for x in (-1, tile_w):
            three = [af[pl.ds(COL_HALO + x + c - 1, 8, wide)] for c in range(3)]
            lo_half.append(jnp.where(lane < 64, three[0], pltpu.roll(three[1], 64, 1)))
            hi_half.append(three[2])
        xe[slot, k, :, 0:LANES] = jnp.concatenate(lo_half, axis=0).astype(BF16)
        xe[slot, k, :, LANES:2 * LANES] = jnp.concatenate(hi_half, axis=0).astype(BF16)

    def conv(src, i0, n, off, weights, xslot, gate, extra=None):
        lo, w_lo = gate * ch, (0 if gate == 2 else gate * ch)
        acc = None
        for c in (1, 0, 2):
            for a in range(3):
                lhs = src(c, pl.ds(i0 + a - 1 - off, n)).reshape(n * tile_w, ch)
                if extra is not None:
                    ends = [cb[3 * side + c, pl.ds(i0 + a - 1 + 8, 8), :] for side in range(2)]
                    lhs = jnp.concatenate([lhs, jnp.concatenate(ends, axis=0).astype(BF16)], axis=0)
                part = jnp.dot(lhs, weights[a, c, :, w_lo:w_lo + ch], preferred_element_type=F32)
                acc = part if acc is None else acc + part
        lhs = xp[xslot, pl.ds(i0 + 1, n)].reshape(n * tile_w, ch)
        if extra is not None:
            lhs = jnp.concatenate([lhs, xe[xslot, extra]], axis=0)
        acc = acc + jnp.dot(lhs, wx[:, lo:lo + ch], preferred_element_type=F32)
        return acc + bv[:, lo:lo + ch]

    for copy in loads:
        copy.wait()
    for k in range(n_chunks):
        i0, n = n_ranges[k]
        for i in range(i0, i0 + n):
            publish(0, i, h32[i], k)
        start_sends(k, 0, True)
    for m, (ok, copy) in enumerate(f_descs):
        src, dst = f_copies[m][1], f_copies[f_recv_index[m]][2]

        @pl.when(ok)
        def _(copy=copy, m=m, src=src, dst=dst):
            copy.wait_send()
            remote(src, dst, fsend.at[m], frecv.at[m], right_dev).wait_recv()
    for k in range(n_chunks):
        build_x(0, 0, k)
    for copy in weight_loads:
        copy.wait()

    def out_copy(t, slot, i):
        return pltpu.make_async_copy(hb.at[slot, 1, i + 2], h_seq.at[t, 0, phys(i)], osem.at[slot, i])

    def step(t, carry):
        now = lax.rem(t, 2)
        new = 1 - now
        more = t < steps - 1
        for k in range(n_chunks):
            if k == 0:
                arrive_cols(now, 0)
                arrive_rows(now, 0)
            if k + 1 < n_chunks:
                arrive_cols(now, k + 1)
            else:
                arrive_rows(now, 1)
            i0, n = r_ranges[k]
            acc = conv(lambda c, rows: hb[now, c, rows], i0, n, -2, wzr, now, 1, extra=k)
            if k > 0:
                start_sends(k - 1, new, more)
            gate = sigmoid(acc)
            ends = gate[n * tile_w:]
            ends_l = ends[0:8] * cb[1, pl.ds(i0 + 8, 8), :]
            ends_r = ends[8:16] * cb[4, pl.ds(i0 + 8, 8), :]
            for j in range(n):
                i = i0 + j
                old = hf[now, 0] if i == -1 else hl[now, 1] if i == tile_h else h32[i]
                v = gate[j * tile_w:(j + 1) * tile_w] * old
                rb[1, i + 1] = v.astype(BF16)
                rb[0, i + 1] = jnp.where(sub48 == 0, ends_l[j:j + 1], pltpu.roll(v, 1, 0)).astype(BF16)
                rb[2, i + 1] = jnp.where(sub48 == tile_w - 1, ends_r[j:j + 1], pltpu.roll(v, tile_w - 1, 0)).astype(BF16)
            i0, n = n_ranges[k]
            zb[pl.ds(0, n * tile_w)] = sigmoid(conv(lambda c, rows: hb[now, c, rows], i0, n, -2, wzr, now, 0))

            build_x(jnp.minimum(t + 1, steps - 1), new, k)
            cand = jnp.tanh(conv(lambda c, rows: rb[c, rows], i0, n, -1, wn, now, 2))
            wait_sends(k, now)
            for i in range(i0, i0 + n):
                @pl.when(t >= 2)
                def _(i=i):
                    out_copy(t, new, i).wait()
            for j in range(n):
                i = i0 + j
                mix = cand[j * tile_w:(j + 1) * tile_w]
                v = mix + zb[pl.ds(j * tile_w, tile_w)] * (h32[i] - mix)
                h32[i] = v
                publish(new, i, v, k)
            for i in range(i0, i0 + n):
                out_copy(t, new, i).start()
        start_sends(n_chunks - 1, new, more)
        return carry

    lax.fori_loop(0, steps, step, 0)
    finals = [pltpu.make_async_copy(h32.at[i], h_last.at[0, phys(i)], lsem.at[i]) for i in range(tile_h)]
    for copy in finals:
        copy.start()
    for slot in range(2):
        for i in range(tile_h):
            out_copy(0, slot, i).wait()
    for copy in finals:
        copy.wait()


def solution(mesh):
    n_rows, n_cols = mesh.shape["rows"], mesh.shape["cols"]
    frame_spec = P(None, "batch", "rows", "cols", None)
    state_spec = P("batch", "rows", "cols", None)

    def local_fn(frames, h_init, w_x, w_hzr, w_hn, gate_bias):
        steps, _, tile_h, tile_w, cin = frames.shape
        ch = h_init.shape[-1]
        dims = (steps, tile_h, tile_w, cin, ch)
        vm = pltpu.VMEM
        dma = pltpu.SemaphoreType.DMA
        kk = len(CHUNKS)
        wide = tile_w + 2 * COL_HALO
        scratch = [
            vm((3, 3, ch, 2 * ch), BF16), vm((3, 3, ch, ch), BF16), vm((256, 3 * ch), BF16), vm((1, 3 * ch), F32),
            vm((tile_h, steps, cin, tile_w), BF16), vm((tile_h + 4, wide, LANES), BF16),
            vm((2, 3, tile_h + 4, tile_w, ch), BF16), vm((3, tile_h + 2, tile_w, ch), BF16),
            vm((2, tile_h + 2, tile_w, ch), BF16), vm((2, kk, 16, ch), BF16), vm((8 * wide, LANES), F32),
            vm((tile_h, tile_w, ch), F32), vm((max(CHUNKS) * tile_w, ch), F32),
            vm((2, 2, tile_w, ch), F32), vm((2, 2, tile_w, ch), F32),
            vm((kk, 4, 8, ch), F32), vm((2, 2, kk, 2, 8, ch), F32), vm((2, 4, 2, 8, ch), F32), vm((6, 48, ch), F32),
            dma((3, tile_h)), dma((14,)), dma((14,)), dma((2, kk)), dma((2, 2, kk)), dma((4,)), dma((2, 4)),
            dma((2,)), dma((2, 2)), dma((2, tile_h)), dma((tile_h,)),
        ]

        def body(*refs):
            kernel_body(n_cols, n_rows, dims, *refs)

        return pl.pallas_call(
            body,
            out_shape=(jax.ShapeDtypeStruct((steps, 1, tile_h, tile_w, ch), BF16), jax.ShapeDtypeStruct((1, tile_h, tile_w, ch), F32)),
            in_specs=[pl.BlockSpec(memory_space=pl.ANY)] * 6,
            out_specs=(pl.BlockSpec(memory_space=pl.ANY),) * 2,
            scratch_shapes=scratch,
            compiler_params=pltpu.CompilerParams(collective_id=0, has_side_effects=True, vmem_limit_bytes=56 * 1024 * 1024),
            name="convgru",
        )(jnp.swapaxes(frames, 3, 4), h_init, w_x, w_hzr, w_hn, gate_bias.reshape(1, -1))

    return jax.shard_map(local_fn, mesh=mesh, in_specs=(frame_spec, state_spec, P(), P(), P(), P()), out_specs=(frame_spec, state_spec), check_vma=False)
```

time: 441 us -> 87.3 us (0.20); the launches traced: 432 us -> 87.1 us
  starting transfers between devices: 195 us -> 0 us
  local copies, waits for them, and re-layouts: 96.1 us -> 7.21 us
  Pallas kernels: 0 us -> 79.3 us
  matrix products: 71.3 us -> 0 us
  other arithmetic: 41.8 us -> 0 us
  waiting for transfers between devices: 24.9 us -> 0 us
    ppermute x68 -> x0, starting transfers between devices: 195 us -> none  [the longest x17 76.8 us: with_halo(): lax.ppermute(tall_tile[..., tile_w - width:, :], 'cols', right_pairs)]
    pallas_call x0 -> x1, Pallas kernels: none -> 79.3 us  [local_fn(): pl.pallas_call(body, out_shape=(jax.ShapeDtypeStruct((steps, 1, tile_h, t...]
    dot_general x24 -> x0, matrix products: 71.3 us -> none  [im2col_conv(): jnp.einsum('...k,kg->...g', patches, w_mat, preferred_element_type=jnp.fl...]
    while x152 -> x0, local copies, waits for them, and re-layouts: 31.5 us -> none
    concatenate x25 -> x0, local copies, waits for them, and re-layouts: 28.2 us -> none  [the longest x24 28.2 us: im2col_conv(): patches = jnp.concatenate(tap_list, axis=-1)]
    ppermute x68 -> x0, waiting for transfers between devices: 24.9 us -> none  [the longest x17 12.1 us: with_halo(): lax.ppermute(tall_tile[..., tile_w - width:, :], 'cols', right_pairs)]
    concatenate x33 -> x0, other arithmetic: 24.6 us -> none  [the longest x17 18.3 us: with_halo(): return jnp.concatenate([from_left, tall_tile, from_right], axis=-2)]
    slice x26 -> x0, local copies, waits for them, and re-layouts: 18.1 us -> none  [the longest x8 12.7 us: im2col_conv(): padded[..., row_off:row_off + out_h, col_off:col_off + out_w, :]]
  transfers between devices with their start and end apart: 68 -> 0, of which waited for: 18 -> 0; matrix products, arithmetic and copies ran while one was open for 14% -> 0% of each run, Pallas kernels for 0% -> 0%
where the time goes in v1:
time: 87.3 us; the launch traced here: 87.1 us
  Pallas kernels  79.3 us (91%)
  local copies, waits for them, and re-layouts  7.21 us (8%)
    pallas_call x1, Pallas kernels, local_fn(): pl.pallas_call(body, out_shape=(jax.ShapeDtypeStruct((steps, 1, tile_h, t...  79.3 us
    unnamed x4, local copies, waits for them, and re-layouts  5.94 us

profile of v1, /device:TPU:0, one launch (start us, length us, event | category | flops | bytes accessed | tf_op | source)
XLA Modules:
  0.0 87.1 jit_solution(12778231006549531511)
XLA Ops:
  0.6 1.3 %reshape.7.refs_5_ = f32[1,768]{1,0:T(1,128)} reshape(f32[768]{0:T(1024)} %param.11) | data formatting | bytes 6144 | tf_op jit(solution)/shard_map/reshape | solution.py:361
  1.9 79.3 %convgru.1 = (bf16[8,1,24,48,256]{4,3,2,1,0:T(8,128)(2,1)}, f32[1,24,48,256]{3,2,1,0:T(8,128)}) custom-call(bf16[8,1,24,16,48]{4,3,2,1,0:T(8,128)(2,1)} %bitcast.1, f32[1,24,48,256]{3,2,1,0:T(8,128)} %refs_1_.1, bf16[3,3,16,768]{3,2,1,0:T(8,128)(2,1)} %refs_2_.1, bf16[3,3,256,512]{3,2,1,0:T(8,128)(2,1)} %refs_3_.1, bf16[3,3,256,256]{3,2,1,0:T(8,128)(2,1)} %refs_4_.1, ...), custom_call_target="tpu_custom_call" | custom-call | tf_op jit(solution)/shard_map/convgru/pallas_call | solution.py:353
  81.2 0.0 copy-start
  81.2 4.9 %copy.10 = bf16[8,1,24,48,256]{4,3,2,1,0:T(8,128)(2,1)} copy(bf16[8,1,24,48,256]{4,3,2,1,0:T(8,128)(2,1)} %get-tuple-element.4) | data formatting | bytes 9437184
  86.1 0.0 copy-done
  86.1 1.0 %copy.11 = f32[1,24,48,256]{3,2,1,0:T(8,128)} copy(f32[1,24,48,256]{3,2,1,0:T(8,128)S(1)} %copy-done) | data formatting | bytes 2359296
Async XLA Ops:
  81.2 4.9 %copy-start = (f32[1,24,48,256]{3,2,1,0:T(8,128)S(1)}, f32[1,24,48,256]{3,2,1,0:T(8,128)}, u32[]{:S(2)}) copy-start(f32[1,24,48,256]{3,2,1,0:T(8,128)} %get-tuple-element.5) | copy-start | bytes 3538948

commit v2 on v1

--- a/solution.py
+++ b/solution.py
@@ -10,7 +10,8 @@
 MESH = pl.DeviceIdType.MESH
 LANES = 128
 COL_HALO = 16
-CHUNKS = (6, 6, 6, 6)
+CHUNKS = (6,) * 4
+UNROLL = 2
 NAMES = ("batch", "cols", "rows")
 
 
@@ -124,35 +125,49 @@
         def _(copy=copy):
             copy.start()
 
-    def col_sends(k, slot):
-        out = [(has_left, remote(cs.at[k, pl.ds(0, 2)], cr.at[slot, 1, k], csend.at[0, k], crecv.at[slot, 1, k], left_dev)),
-               (has_right, remote(cs.at[k, pl.ds(2, 2)], cr.at[slot, 0, k], csend.at[1, k], crecv.at[slot, 0, k], right_dev))]
+    def chunk_sends(k, slot):
+        to_left = cs.at[slot, k, 0]
+        to_right = cs.at[slot, k, 1]
+        out = [(has_left, remote(to_left, cr.at[slot, 1, k], csend.at[slot, 0, k], crecv.at[slot, 1, k], left_dev)),
+               (has_right, remote(to_right, cr.at[slot, 0, k], csend.at[slot, 1, k], crecv.at[slot, 0, k], right_dev))]
+        for edge, q in ((0, 0), (n_chunks - 1, 2)):
+            if k == edge:
+                out.append((corner_ok[q], remote(to_left, kr.at[slot, q + 1], ksend.at[slot, q], krecv.at[slot, q + 1], corner_dev[q])))
+                out.append((corner_ok[q + 1], remote(to_right, kr.at[slot, q], ksend.at[slot, q + 1], krecv.at[slot, q], corner_dev[q + 1])))
+        return out
+
+    def row_send(k, slot):
         if k == 0:
-            out.append((has_first, remote(h32.at[pl.ds(0, 2)], hf.at[slot], vsend.at[0], vrecv.at[slot, 0], first_dev)))
-            out.append((corner_ok[0], remote(cs.at[k, pl.ds(0, 2)], kr.at[slot, 1], ksend.at[0], krecv.at[slot, 1], corner_dev[0])))
-            out.append((corner_ok[1], remote(cs.at[k, pl.ds(2, 2)], kr.at[slot, 0], ksend.at[1], krecv.at[slot, 0], corner_dev[1])))
-        if k == n_chunks - 1:
-            out.append((has_last, remote(h32.at[pl.ds(tile_h - 2, 2)], hl.at[slot], vsend.at[1], vrecv.at[slot, 1], last_dev)))
-            out.append((corner_ok[2], remote(cs.at[k, pl.ds(0, 2)], kr.at[slot, 3], ksend.at[2], krecv.at[slot, 3], corner_dev[2])))
-            out.append((corner_ok[3], remote(cs.at[k, pl.ds(2, 2)], kr.at[slot, 2], ksend.at[3], krecv.at[slot, 2], corner_dev[3])))
-        return out
+            return has_first, remote(h32.at[pl.ds(0, 2)], hf.at[slot], vsend.at[0], vrecv.at[slot, 0], first_dev)
+        return has_last, remote(h32.at[pl.ds(tile_h - 2, 2)], hl.at[slot], vsend.at[1], vrecv.at[slot, 1], last_dev)
 
     def start_sends(k, slot, more):
-        for ok, copy in col_sends(k, slot):
+        copies = chunk_sends(k, slot)
+        if k in (0, n_chunks - 1):
+            copies.append(row_send(k, slot))
+        for ok, copy in copies:
             @pl.when(both(ok, more))
             def _(copy=copy):
                 copy.start()
 
-    def wait_sends(k, slot):
-        for ok, copy in col_sends(k, slot):
-            @pl.when(ok)
-            def _(copy=copy):
-                copy.wait_send()
+    def wait_chunk_sends(slot, cond):
+        for k in range(n_chunks):
+            for ok, copy in chunk_sends(k, slot):
+                @pl.when(both(ok, cond))
+                def _(copy=copy):
+                    copy.wait_send()
+
+    def wait_row_send(k, slot):
+        ok, copy = row_send(k, slot)
+
+        @pl.when(ok)
+        def _():
+            copy.wait_send()
 
     def wait_if(ok, dst, sem, src):
         @pl.when(ok)
         def _():
-            remote(src, dst, csend.at[0, 0], sem, right_dev).wait_recv()
+            remote(src, dst, csend.at[0, 0, 0], sem, right_dev).wait_recv()
 
     sub48 = lax.broadcasted_iota(jnp.int32, (tile_w, ch), 0)
     sub16 = lax.broadcasted_iota(jnp.int32, (16, ch), 0)
@@ -165,37 +180,42 @@
         hb[slot, 0, i + 2] = pltpu.roll(v, 1, 0).astype(BF16)
         hb[slot, 2, i + 2] = pltpu.roll(v, tile_w - 1, 0).astype(BF16)
         j = i - starts[k]
-        for q, x in enumerate((0, 1, tile_w - 2, tile_w - 1)):
-            cs[k, q, pl.ds(j, 1), :] = v[x:x + 1]
+        for side, m, x in ((0, 0, 0), (0, 1, 1), (1, 0, tile_w - 2), (1, 1, tile_w - 1)):
+            cs[slot, k, side, pl.ds(8 * m + j, 1), :] = v[x:x + 1]
         cb[2, pl.ds(i + 8, 1), :] = v[0:1]
         cb[3, pl.ds(i + 8, 1), :] = v[tile_w - 1:tile_w]
 
-    def arrive_cols(slot, k):
-        wait_if(has_left, cr.at[slot, 0, k], crecv.at[slot, 0, k], cs.at[k, pl.ds(0, 2)])
-        wait_if(has_right, cr.at[slot, 1, k], crecv.at[slot, 1, k], cs.at[k, pl.ds(0, 2)])
+    def wait_cols(slot, k):
+        wait_if(has_left, cr.at[slot, 0, k], crecv.at[slot, 0, k], cs.at[slot, k, 0])
+        wait_if(has_right, cr.at[slot, 1, k], crecv.at[slot, 1, k], cs.at[slot, k, 0])
+
+    def place_cols(slot, k):
         i0, n = n_ranges[k]
         for side in range(2):
             for m in range(2):
-                cb[4 * side + m, pl.ds(i0 + 8, n), :] = cr[slot, side, k, m, 0:n, :]
+                cb[4 * side + m, pl.ds(i0 + 8, n), :] = cr[slot, side, k, 8 * m:8 * m + n, :]
         for i in range(i0, i0 + n):
             old = hb[slot, 0, i + 2, 0:16].astype(F32)
             hb[slot, 0, i + 2, 0:16] = jnp.where(sub16 == 0, row_of(1, i), old).astype(BF16)
             old = hb[slot, 2, i + 2, tile_w - 16:tile_w].astype(F32)
             hb[slot, 2, i + 2, tile_w - 16:tile_w] = jnp.where(sub16 == 15, row_of(4, i), old).astype(BF16)
 
-    def arrive_rows(slot, last):
+    def wait_rows(slot, last):
         src, ok = (hl, has_last) if last else (hf, has_first)
         wait_if(ok, src.at[slot], vrecv.at[slot, last], h32.at[pl.ds(0, 2)])
         for m in range(2):
             q = 2 * last + m
-            wait_if(corner_ok[q], kr.at[slot, q], krecv.at[slot, q], cs.at[0, pl.ds(0, 2)])
+            wait_if(corner_ok[q], kr.at[slot, q], krecv.at[slot, q], cs.at[slot, 0, 0])
+
+    def place_rows(slot, last):
+        src = hl if last else hf
         for depth in range(2):
             i = tile_h + depth if last else -1 - depth
             m = 1 - depth if last else depth
             j = CHUNKS[-1] - 1 - depth if last else depth
             for x in range(2):
-                cb[x, pl.ds(i + 8, 1), :] = kr[slot, 2 * last, x, j:j + 1, :]
-                cb[4 + x, pl.ds(i + 8, 1), :] = kr[slot, 2 * last + 1, x, j:j + 1, :]
+                cb[x, pl.ds(i + 8, 1), :] = kr[slot, 2 * last, 8 * x + j:8 * x + j + 1, :]
+                cb[4 + x, pl.ds(i + 8, 1), :] = kr[slot, 2 * last + 1, 8 * x + j:8 * x + j + 1, :]
             v = src[slot, m]
             cb[2, pl.ds(i + 8, 1), :] = v[0:1]
             cb[3, pl.ds(i + 8, 1), :] = v[tile_w - 1:tile_w]
@@ -224,14 +244,14 @@
         xe[slot, k, :, 0:LANES] = jnp.concatenate(lo_half, axis=0).astype(BF16)
         xe[slot, k, :, LANES:2 * LANES] = jnp.concatenate(hi_half, axis=0).astype(BF16)
 
-    def conv(src, i0, n, off, weights, xslot, gate, extra=None):
+    def conv(src, i0, n, off, weights, xslot, gate, extra=None, e_lo=0):
         lo, w_lo = gate * ch, (0 if gate == 2 else gate * ch)
         acc = None
         for c in (1, 0, 2):
             for a in range(3):
                 lhs = src(c, pl.ds(i0 + a - 1 - off, n)).reshape(n * tile_w, ch)
                 if extra is not None:
-                    ends = [cb[3 * side + c, pl.ds(i0 + a - 1 + 8, 8), :] for side in range(2)]
+                    ends = [cb[3 * side + c, pl.ds(e_lo + a - 1 + 8, 8), :] for side in range(2)]
                     lhs = jnp.concatenate([lhs, jnp.concatenate(ends, axis=0).astype(BF16)], axis=0)
                 part = jnp.dot(lhs, weights[a, c, :, w_lo:w_lo + ch], preferred_element_type=F32)
                 acc = part if acc is None else acc + part
@@ -239,7 +259,7 @@
         if extra is not None:
             lhs = jnp.concatenate([lhs, xe[xslot, extra]], axis=0)
         acc = acc + jnp.dot(lhs, wx[:, lo:lo + ch], preferred_element_type=F32)
-        return acc + bv[:, lo:lo + ch]
+        return acc + bv[lo:lo + ch].reshape(1, ch)
 
     for copy in loads:
         copy.wait()
@@ -263,55 +283,91 @@
     def out_copy(t, slot, i):
         return pltpu.make_async_copy(hb.at[slot, 1, i + 2], h_seq.at[t, 0, phys(i)], osem.at[slot, i])
 
-    def step(t, carry):
-        now = lax.rem(t, 2)
+    def halves(i0, n):
+        return (i0, n - n // 2), (i0 + n - n // 2, n // 2)
+
+    def meet(t, now, k):
         new = 1 - now
-        more = t < steps - 1
-        for k in range(n_chunks):
-            if k == 0:
-                arrive_cols(now, 0)
-                arrive_rows(now, 0)
-            if k + 1 < n_chunks:
-                arrive_cols(now, k + 1)
-            else:
-                arrive_rows(now, 1)
-            i0, n = r_ranges[k]
-            acc = conv(lambda c, rows: hb[now, c, rows], i0, n, -2, wzr, now, 1, extra=k)
-            if k > 0:
-                start_sends(k - 1, new, more)
-            gate = sigmoid(acc)
-            ends = gate[n * tile_w:]
-            ends_l = ends[0:8] * cb[1, pl.ds(i0 + 8, 8), :]
-            ends_r = ends[8:16] * cb[4, pl.ds(i0 + 8, 8), :]
+        if k == 0:
+            start_sends(n_chunks - 1, now, both(t > 0, True))
+            last_outs(t - 1, now, n_chunks - 1, t > 0)
+            free_slot(t, now)
+            wait_cols(now, 0)
+            wait_rows(now, 0)
+            wait_row_send(0, now)
+        else:
+            start_sends(k - 1, new, t < steps - 1)
+            last_outs(t, new, k - 1, True)
+        if k + 1 < n_chunks:
+            wait_cols(now, k + 1)
+        else:
+            wait_rows(now, 1)
+            wait_row_send(n_chunks - 1, now)
+        if k == 0:
+            place_cols(now, 0)
+            place_rows(now, 0)
+        if k + 1 < n_chunks:
+            place_cols(now, k + 1)
+        else:
+            place_rows(now, 1)
+
+    def last_outs(t, slot, k, cond):
+        for i in range(n_ranges[k][0], sum(n_ranges[k])):
+            @pl.when(cond)
+            def _(i=i):
+                out_copy(t, slot, i).start()
+
+    def free_slot(t, now):
+        new = 1 - now
+        wait_chunk_sends(new, t >= 1)
+        for i in range(tile_h):
+            @pl.when(t >= 2)
+            def _(i=i):
+                out_copy(t, new, i).wait()
+
+    def stretch(t, now, k):
+        new = 1 - now
+        meet(t, now, k)
+        r_lo, r_n = r_ranges[k]
+        parts = halves(r_lo, r_n)
+        accs = [conv(lambda c, rows: hb[now, c, rows], i0, n, -2, wzr, now, 1, extra=k if h == 1 else None, e_lo=r_lo) for h, (i0, n) in enumerate(parts)]
+        gates = [sigmoid(acc) for acc in accs]
+        ends = gates[1][parts[1][1] * tile_w:]
+        ends_l = ends[0:8] * cb[1, pl.ds(r_lo + 8, 8), :]
+        ends_r = ends[8:16] * cb[4, pl.ds(r_lo + 8, 8), :]
+        for (i0, n), gate in zip(parts, gates):
             for j in range(n):
                 i = i0 + j
+                e = i - r_lo
                 old = hf[now, 0] if i == -1 else hl[now, 1] if i == tile_h else h32[i]
                 v = gate[j * tile_w:(j + 1) * tile_w] * old
                 rb[1, i + 1] = v.astype(BF16)
-                rb[0, i + 1] = jnp.where(sub48 == 0, ends_l[j:j + 1], pltpu.roll(v, 1, 0)).astype(BF16)
-                rb[2, i + 1] = jnp.where(sub48 == tile_w - 1, ends_r[j:j + 1], pltpu.roll(v, tile_w - 1, 0)).astype(BF16)
-            i0, n = n_ranges[k]
-            zb[pl.ds(0, n * tile_w)] = sigmoid(conv(lambda c, rows: hb[now, c, rows], i0, n, -2, wzr, now, 0))
-
-            build_x(jnp.minimum(t + 1, steps - 1), new, k)
-            cand = jnp.tanh(conv(lambda c, rows: rb[c, rows], i0, n, -1, wn, now, 2))
-            wait_sends(k, now)
-            for i in range(i0, i0 + n):
-                @pl.when(t >= 2)
-                def _(i=i):
-                    out_copy(t, new, i).wait()
+                rb[0, i + 1] = jnp.where(sub48 == 0, ends_l[e:e + 1], pltpu.roll(v, 1, 0)).astype(BF16)
+                rb[2, i + 1] = jnp.where(sub48 == tile_w - 1, ends_r[e:e + 1], pltpu.roll(v, tile_w - 1, 0)).astype(BF16)
+        parts = halves(*n_ranges[k])
+        accs = [conv(lambda c, rows: hb[now, c, rows], i0, n, -2, wzr, now, 0) for i0, n in parts]
+        for (i0, n), acc in zip(parts, accs):
+            zb[pl.ds((i0 - n_ranges[k][0]) * tile_w, n * tile_w)] = sigmoid(acc)
+        build_x(jnp.minimum(t + 1, steps - 1), new, k)
+        accs = [conv(lambda c, rows: rb[c, rows], i0, n, -1, wn, now, 2) for i0, n in parts]
+        for (i0, n), acc in zip(parts, accs):
+            cand = jnp.tanh(acc)
             for j in range(n):
                 i = i0 + j
                 mix = cand[j * tile_w:(j + 1) * tile_w]
-                v = mix + zb[pl.ds(j * tile_w, tile_w)] * (h32[i] - mix)
+                v = mix + zb[pl.ds((i - n_ranges[k][0]) * tile_w, tile_w)] * (h32[i] - mix)
                 h32[i] = v
                 publish(new, i, v, k)
-            for i in range(i0, i0 + n):
-                out_copy(t, new, i).start()
-        start_sends(n_chunks - 1, new, more)
+
+    def body(p, carry):
+        for s in range(UNROLL):
+            for k in range(n_chunks):
+                stretch(UNROLL * p + s, s % 2, k)
         return carry
 
-    lax.fori_loop(0, steps, step, 0)
+    lax.fori_loop(0, steps // UNROLL, body, 0)
+    wait_chunk_sends((steps - 1) % 2, True)
+    last_outs(steps - 1, 0, n_chunks - 1, True)
     finals = [pltpu.make_async_copy(h32.at[i], h_last.at[0, phys(i)], lsem.at[i]) for i in range(tile_h)]
     for copy in finals:
         copy.start()
@@ -336,14 +392,14 @@
         kk = len(CHUNKS)
         wide = tile_w + 2 * COL_HALO
         scratch = [
-            vm((3, 3, ch, 2 * ch), BF16), vm((3, 3, ch, ch), BF16), vm((256, 3 * ch), BF16), vm((1, 3 * ch), F32),
+            vm((3, 3, ch, 2 * ch), BF16), vm((3, 3, ch, ch), BF16), vm((256, 3 * ch), BF16), vm((3 * ch,), F32),
             vm((tile_h, steps, cin, tile_w), BF16), vm((tile_h + 4, wide, LANES), BF16),
             vm((2, 3, tile_h + 4, tile_w, ch), BF16), vm((3, tile_h + 2, tile_w, ch), BF16),
             vm((2, tile_h + 2, tile_w, ch), BF16), vm((2, kk, 16, ch), BF16), vm((8 * wide, LANES), F32),
             vm((tile_h, tile_w, ch), F32), vm((max(CHUNKS) * tile_w, ch), F32),
             vm((2, 2, tile_w, ch), F32), vm((2, 2, tile_w, ch), F32),
-            vm((kk, 4, 8, ch), F32), vm((2, 2, kk, 2, 8, ch), F32), vm((2, 4, 2, 8, ch), F32), vm((6, 48, ch), F32),
-            dma((3, tile_h)), dma((14,)), dma((14,)), dma((2, kk)), dma((2, 2, kk)), dma((4,)), dma((2, 4)),
+            vm((2, kk, 2, 16, ch), F32), vm((2, 2, kk, 16, ch), F32), vm((2, 4, 16, ch), F32), vm((6, 48, ch), F32),
+            dma((3, tile_h)), dma((14,)), dma((14,)), dma((2, 2, kk)), dma((2, 2, kk)), dma((2, 4)), dma((2, 4)),
             dma((2,)), dma((2, 2)), dma((2, tile_h)), dma((tile_h,)),
         ]
 
@@ -358,6 +414,6 @@
             scratch_shapes=scratch,
             compiler_params=pltpu.CompilerParams(collective_id=0, has_side_effects=True, vmem_limit_bytes=56 * 1024 * 1024),
             name="convgru",
-        )(jnp.swapaxes(frames, 3, 4), h_init, w_x, w_hzr, w_hn, gate_bias.reshape(1, -1))
+        )(jnp.swapaxes(frames, 3, 4), h_init, w_x, w_hzr, w_hn, gate_bias)
 
     return jax.shard_map(local_fn, mesh=mesh, in_specs=(frame_spec, state_spec, P(), P(), P(), P()), out_specs=(frame_spec, state_spec), check_vma=False)

time: 87.3 us -> 69.5 us (0.80)
  Pallas kernels: 79.3 us -> 62.7 us
  local copies, waits for them, and re-layouts: 7.21 us -> 5.94 us
    pallas_call x1, Pallas kernels: 79.3 us -> 62.7 us  [local_fn(): pl.pallas_call(body, out_shape=(jax.ShapeDtypeStruct((steps, 1, tile_h, t...]
    reshape x1 -> x0, local copies, waits for them, and re-layouts: 1.27 us -> none  [local_fn(): gate_bias.reshape(1, -1)]
where the time goes in v2:
time: 69.5 us; the launch traced here: 69.3 us
  Pallas kernels  62.7 us (90%)
  local copies, waits for them, and re-layouts  5.94 us (9%)
    pallas_call x1, Pallas kernels, local_fn(): pl.pallas_call(body, out_shape=(jax.ShapeDtypeStruct((steps, 1, tile_h, t...  62.7 us
    unnamed x4, local copies, waits for them, and re-layouts  5.94 us

profile of v2, /device:TPU:0, one launch (start us, length us, event | category | flops | bytes accessed | tf_op | source)
XLA Modules:
  0.0 69.3 jit_solution(5585856659477540109)
XLA Ops:
  0.6 62.7 %convgru.1 = (bf16[8,1,24,48,256]{4,3,2,1,0:T(8,128)(2,1)}, f32[1,24,48,256]{3,2,1,0:T(8,128)}) custom-call(bf16[8,1,24,16,48]{4,3,2,1,0:T(8,128)(2,1)} %bitcast.1, f32[1,24,48,256]{3,2,1,0:T(8,128)} %refs_1_.1, bf16[3,3,16,768]{3,2,1,0:T(8,128)(2,1)} %refs_2_.1, bf16[3,3,256,512]{3,2,1,0:T(8,128)(2,1)} %refs_3_.1, bf16[3,3,256,256]{3,2,1,0:T(8,128)(2,1)} %refs_4_.1, ...), custom_call_target="tpu_custom_call" | custom-call | tf_op jit(solution)/shard_map/convgru/pallas_call | solution.py:409
  63.4 0.0 copy-start
  63.4 4.9 %copy.10 = bf16[8,1,24,48,256]{4,3,2,1,0:T(8,128)(2,1)} copy(bf16[8,1,24,48,256]{4,3,2,1,0:T(8,128)(2,1)} %get-tuple-element.4) | data formatting | bytes 9437184
  68.3 0.0 copy-done
  68.3 1.0 %copy.11 = f32[1,24,48,256]{3,2,1,0:T(8,128)} copy(f32[1,24,48,256]{3,2,1,0:T(8,128)S(1)} %copy-done) | data formatting | bytes 2359296
Async XLA Ops:
  63.4 4.9 %copy-start = (f32[1,24,48,256]{3,2,1,0:T(8,128)S(1)}, f32[1,24,48,256]{3,2,1,0:T(8,128)}, u32[]{:S(2)}) copy-start(f32[1,24,48,256]{3,2,1,0:T(8,128)} %get-tuple-element.5) | copy-start | bytes 3538948

commit v3 on v2

--- a/solution.py
+++ b/solution.py
@@ -12,6 +12,7 @@
 COL_HALO = 16
 CHUNKS = (6,) * 4
 UNROLL = 2
+VMEM_LIMIT = 40 * 1024 * 1024
 NAMES = ("batch", "cols", "rows")
 
 
@@ -21,7 +22,7 @@
 
 def kernel_body(n_cols, n_rows, dims, frames, h_init, w_x, w_hzr, w_hn, bias, h_seq, h_last,
                 wzr, wn, wx, bv, fv, fp, hb, rb, xp, xe, af, h32, zb, hf, hl, cs, cr, kr, cb,
-                load_sem, fsend, frecv, csend, crecv, ksend, krecv, vsend, vrecv, osem, lsem):
+                load_sem, fsend, frecv, csend, crecv, ksend, krecv, vsend, vrecv):
     steps, tile_h, tile_w, cin, ch = dims
     batch = lax.axis_index("batch")
     col = lax.axis_index("cols")
@@ -280,9 +281,6 @@
     for copy in weight_loads:
         copy.wait()
 
-    def out_copy(t, slot, i):
-        return pltpu.make_async_copy(hb.at[slot, 1, i + 2], h_seq.at[t, 0, phys(i)], osem.at[slot, i])
-
     def halves(i0, n):
         return (i0, n - n // 2), (i0 + n - n // 2, n // 2)
 
@@ -290,14 +288,12 @@
         new = 1 - now
         if k == 0:
             start_sends(n_chunks - 1, now, both(t > 0, True))
-            last_outs(t - 1, now, n_chunks - 1, t > 0)
             free_slot(t, now)
             wait_cols(now, 0)
             wait_rows(now, 0)
             wait_row_send(0, now)
         else:
             start_sends(k - 1, new, t < steps - 1)
-            last_outs(t, new, k - 1, True)
         if k + 1 < n_chunks:
             wait_cols(now, k + 1)
         else:
@@ -311,19 +307,9 @@
         else:
             place_rows(now, 1)
 
-    def last_outs(t, slot, k, cond):
-        for i in range(n_ranges[k][0], sum(n_ranges[k])):
-            @pl.when(cond)
-            def _(i=i):
-                out_copy(t, slot, i).start()
-
     def free_slot(t, now):
         new = 1 - now
         wait_chunk_sends(new, t >= 1)
-        for i in range(tile_h):
-            @pl.when(t >= 2)
-            def _(i=i):
-                out_copy(t, new, i).wait()
 
     def stretch(t, now, k):
         new = 1 - now
@@ -357,6 +343,7 @@
                 mix = cand[j * tile_w:(j + 1) * tile_w]
                 v = mix + zb[pl.ds((i - n_ranges[k][0]) * tile_w, tile_w)] * (h32[i] - mix)
                 h32[i] = v
+                h_seq[t, 0, phys(i)] = v.astype(BF16)
                 publish(new, i, v, k)
 
     def body(p, carry):
@@ -367,15 +354,8 @@
 
     lax.fori_loop(0, steps // UNROLL, body, 0)
     wait_chunk_sends((steps - 1) % 2, True)
-    last_outs(steps - 1, 0, n_chunks - 1, True)
-    finals = [pltpu.make_async_copy(h32.at[i], h_last.at[0, phys(i)], lsem.at[i]) for i in range(tile_h)]
-    for copy in finals:
-        copy.start()
-    for slot in range(2):
-        for i in range(tile_h):
-            out_copy(0, slot, i).wait()
-    for copy in finals:
-        copy.wait()
+    for i in range(tile_h):
+        h_last[0, phys(i)] = h32[i]
 
 
 def solution(mesh):
@@ -400,7 +380,7 @@
             vm((2, 2, tile_w, ch), F32), vm((2, 2, tile_w, ch), F32),
             vm((2, kk, 2, 16, ch), F32), vm((2, 2, kk, 16, ch), F32), vm((2, 4, 16, ch), F32), vm((6, 48, ch), F32),
             dma((3, tile_h)), dma((14,)), dma((14,)), dma((2, 2, kk)), dma((2, 2, kk)), dma((2, 4)), dma((2, 4)),
-            dma((2,)), dma((2, 2)), dma((2, tile_h)), dma((tile_h,)),
+            dma((2,)), dma((2, 2)),
         ]
 
         def body(*refs):
@@ -408,12 +388,12 @@
 
         return pl.pallas_call(
             body,
-            out_shape=(jax.ShapeDtypeStruct((steps, 1, tile_h, tile_w, ch), BF16), jax.ShapeDtypeStruct((1, tile_h, tile_w, ch), F32)),
-            in_specs=[pl.BlockSpec(memory_space=pl.ANY)] * 6,
-            out_specs=(pl.BlockSpec(memory_space=pl.ANY),) * 2,
+            out_shape=(vm((steps, 1, tile_h, tile_w, ch), BF16), vm((1, tile_h, tile_w, ch), F32)),
+            in_specs=[pl.BlockSpec(memory_space=pltpu.HBM)] * 6,
+            out_specs=(pl.BlockSpec(memory_space=vm),) * 2,
             scratch_shapes=scratch,
-            compiler_params=pltpu.CompilerParams(collective_id=0, has_side_effects=True, vmem_limit_bytes=56 * 1024 * 1024),
+            compiler_params=pltpu.CompilerParams(collective_id=0, has_side_effects=True, vmem_limit_bytes=VMEM_LIMIT),
             name="convgru",
-        )(jnp.swapaxes(frames, 3, 4), h_init, w_x, w_hzr, w_hn, gate_bias)
+        )(*[pltpu.with_memory_space_constraint(v, pltpu.HBM) for v in (jnp.swapaxes(frames, 3, 4), h_init, w_x, w_hzr, w_hn, gate_bias)])
 
     return jax.shard_map(local_fn, mesh=mesh, in_specs=(frame_spec, state_spec, P(), P(), P(), P()), out_specs=(frame_spec, state_spec), check_vma=False)

time: 69.5 us -> 64.6 us (0.929)
  local copies, waits for them, and re-layouts: 5.94 us -> 3.2 us
  Pallas kernels: 62.7 us -> 60.6 us
    unnamed x4 -> x2, local copies, waits for them, and re-layouts: 5.94 us -> 3.2 us
    pallas_call x1, Pallas kernels: 62.7 us -> 60.6 us  [local_fn(): pl.pallas_call(body, out_shape=(vm((steps, 1, tile_h, tile_w, ch), BF16),...]
where the time goes in v3:
time: 64.6 us; the launch traced here: 64.4 us
  Pallas kernels  60.6 us (94%)
  local copies, waits for them, and re-layouts  3.2 us (5%)
    pallas_call x1, Pallas kernels, local_fn(): pl.pallas_call(body, out_shape=(vm((steps, 1, tile_h, tile_w, ch), BF16),...  60.6 us
    unnamed x2, local copies, waits for them, and re-layouts  3.2 us

profile of v3, /device:TPU:0, one launch (start us, length us, event | category | flops | bytes accessed | tf_op | source)
XLA Modules:
  0.0 64.4 jit_solution(8757658939422415610)
XLA Ops:
  0.6 60.6 %convgru.1 = (bf16[8,1,24,48,256]{4,3,2,1,0:T(8,128)(2,1)S(1)}, f32[1,24,48,256]{3,2,1,0:T(8,128)S(1)}) custom-call(bf16[8,1,24,16,48]{4,3,2,1,0:T(8,128)(2,1)} %bitcast.1, f32[1,24,48,256]{3,2,1,0:T(8,128)} %refs_1_.1, bf16[3,3,16,768]{3,2,1,0:T(8,128)(2,1)} %refs_2_.1, bf16[3,3,256,512]{3,2,1,0:T(8,128)(2,1)} %refs_3_.1, bf16[3,3,256,256]{3,2,1,0:T(8,128)(2,1)} %refs_4_.1, ...), custom_call_target="tpu_custom_call" | custom-call | tf_op jit(solution)/shard_map/convgru/pallas_call | solution.py:389
  61.2 2.2 %copy.10 = bf16[8,1,24,48,256]{4,3,2,1,0:T(8,128)(2,1)} copy(bf16[8,1,24,48,256]{4,3,2,1,0:T(8,128)(2,1)S(1)} %get-tuple-element.2) | data formatting | bytes 9437184
  63.4 1.0 %copy.11 = f32[1,24,48,256]{3,2,1,0:T(8,128)} copy(f32[1,24,48,256]{3,2,1,0:T(8,128)S(1)} %get-tuple-element.3) | data formatting | bytes 2359296

commit v4 on v3

--- a/solution.py
+++ b/solution.py
@@ -9,9 +9,10 @@
 F32 = jnp.float32
 MESH = pl.DeviceIdType.MESH
 LANES = 128
-COL_HALO = 16
+COL_HALO = 8
 CHUNKS = (6,) * 4
 UNROLL = 2
+AHEAD = 5
 VMEM_LIMIT = 40 * 1024 * 1024
 NAMES = ("batch", "cols", "rows")
 
@@ -21,9 +22,10 @@
 
 
 def kernel_body(n_cols, n_rows, dims, frames, h_init, w_x, w_hzr, w_hn, bias, h_seq, h_last,
-                wzr, wn, wx, bv, fv, fp, hb, rb, xp, xe, af, h32, zb, hf, hl, cs, cr, kr, cb,
+                wzr, wn, wx, bv, fv, fp, fcs, fcr, fkr, hb, rb, xp, xe, af, hraw, h32, zb, hf, hl, cs, cr, kr, cb,
                 load_sem, fsend, frecv, csend, crecv, ksend, krecv, vsend, vrecv):
     steps, tile_h, tile_w, cin, ch = dims
+    edge_cells = ((0, 0, 0), (0, 1, 1), (1, 0, tile_w - 2), (1, 1, tile_w - 1))
     batch = lax.axis_index("batch")
     col = lax.axis_index("cols")
     row = lax.axis_index("rows")
@@ -58,10 +60,12 @@
     def remote(src, dst, s_sem, r_sem, dev):
         return pltpu.make_async_remote_copy(src_ref=src, dst_ref=dst, send_sem=s_sem, recv_sem=r_sem, device_id=dev, device_id_type=MESH)
 
-    loads = []
-    for i in range(tile_h):
-        loads.append(pltpu.make_async_copy(h_init.at[0, phys(i)], h32.at[i], load_sem.at[0, i]))
-    frame_loads = [pltpu.make_async_copy(frames.at[:, 0, phys(i)], fv.at[i], load_sem.at[1, i]) for i in range(tile_h)]
+    def chunk_rows(k):
+        i0, n = n_ranges[k]
+        return pl.ds(i0 + flip * (tile_h - n - 2 * i0), n)
+
+    loads = [pltpu.make_async_copy(h_init.at[0, chunk_rows(k)], hraw.at[chunk_rows(k)], load_sem.at[0, k]) for k in range(n_chunks)]
+    frame_loads = [pltpu.make_async_copy(frames.at[:, 0], fv, load_sem.at[1, 0])]
     weight_loads = []
     for a in range(3):
         la = a + flip * (2 - 2 * a)
@@ -71,7 +75,7 @@
             dst = wx.at[pl.ds(pl.multiple_of(64 * c + cin * la, cin), cin)]
             weight_loads.append(pltpu.make_async_copy(w_x.at[a, c], dst, load_sem.at[2, 6 + 3 * a + c]))
     weight_loads.append(pltpu.make_async_copy(bias, bv, load_sem.at[2, 15]))
-    for copy in frame_loads + loads + weight_loads:
+    for copy in loads + frame_loads + weight_loads:
         copy.start()
 
     hf[...] = jnp.zeros_like(hf)
@@ -79,8 +83,12 @@
     cr[...] = jnp.zeros_like(cr)
     kr[...] = jnp.zeros_like(kr)
     cb[...] = jnp.zeros_like(cb)
-    cs[...] = jnp.zeros_like(cs)
-    fp[...] = jnp.zeros_like(fp)
+    fcr[...] = jnp.zeros_like(fcr)
+    fkr[...] = jnp.zeros_like(fkr)
+    for i in (0, 1, tile_h + 2, tile_h + 3):
+        fp[i] = jnp.zeros_like(fp[i])
+    for lo in (0, COL_HALO + tile_w):
+        fp[:, lo:lo + COL_HALO, :] = jnp.zeros((tile_h + 4, COL_HALO, LANES), F32)
     for lo, hi in ((48, 64), (112, 128), (176, 256)):
         wx[lo:hi] = jnp.zeros((hi - lo, 3 * ch), BF16)
 
@@ -92,45 +100,47 @@
         @pl.when(ok)
         def _(dev=dev):
             pl.semaphore_signal(barrier, inc=1, device_id=dev, device_id_type=MESH)
-    pl.semaphore_wait(barrier, count)
-
     lane = lax.broadcasted_iota(jnp.int32, (1, LANES), 1)
 
-    for copy in frame_loads:
-        copy.wait()
     own_c = pl.ds(COL_HALO, tile_w)
-    for i in range(tile_h):
-        fp[i + 2, own_c] = fv[i].reshape(steps * cin, tile_w).astype(F32).T.astype(BF16)
-
-    lo_c = pl.ds(0, COL_HALO)
-    hi_c = pl.ds(COL_HALO + tile_w, COL_HALO)
-    own_lo = pl.ds(COL_HALO, COL_HALO)
-    own_hi = pl.ds(tile_w, COL_HALO)
-    f_copies = []
-    own_r = pl.ds(2, tile_h)
-    f_copies.append((has_left, fp.at[own_r, own_lo], fp.at[own_r, hi_c], left_dev))
-    f_copies.append((has_right, fp.at[own_r, own_hi], fp.at[own_r, lo_c], right_dev))
-    for ok, okl, okr, dev, cdl, cdr, rows in (
-            (has_first, corner_ok[0], corner_ok[1], first_dev, corner_dev[0], corner_dev[1], ((2, 1), (3, 0))),
-            (has_last, corner_ok[2], corner_ok[3], last_dev, corner_dev[2], corner_dev[3], ((tile_h + 1, tile_h + 2), (tile_h, tile_h + 3)))):
-        for src, dst in rows:
-            f_copies.append((ok, fp.at[src, own_c], fp.at[dst, own_c], dev))
-            f_copies.append((okl, fp.at[src, own_lo], fp.at[dst, hi_c], cdl))
-            f_copies.append((okr, fp.at[src, own_hi], fp.at[dst, lo_c], cdr))
-    f_recv_index = [1, 0]
-    for g in range(4):
-        f_recv_index += [2 + 3 * g, 4 + 3 * g, 3 + 3 * g]
-    f_descs = [(ok, remote(s, d, fsend.at[m], frecv.at[f_recv_index[m]], dev)) for m, (ok, s, d, dev) in enumerate(f_copies)]
-    for ok, copy in f_descs:
-        @pl.when(ok)
-        def _(copy=copy):
-            copy.start()
+
+    def pack_frames():
+        for i in range(tile_h):
+            v = fv[:, phys(i)].reshape(steps * cin, tile_w).astype(F32).T
+            fp[i + 2, own_c] = v
+            for side, m, x in edge_cells:
+                fcs[side, m, pl.ds(i, 1), :] = v[x:x + 1]
+
+    def frame_copies():
+        out = [(has_left, remote(fcs.at[0], fcr.at[1], fsend.at[0], frecv.at[1], left_dev), fcr.at[0], frecv.at[0]),
+               (has_right, remote(fcs.at[1], fcr.at[0], fsend.at[1], frecv.at[0], right_dev), fcr.at[1], frecv.at[1])]
+        rows = ((has_first, first_dev, 2, 1), (has_first, first_dev, 3, 0), (has_last, last_dev, tile_h + 1, tile_h + 2), (has_last, last_dev, tile_h, tile_h + 3))
+        for m, (ok, dev, src, dst) in enumerate(rows):
+            out.append((ok, remote(fp.at[src, own_c], fp.at[dst, own_c], fsend.at[2 + m], frecv.at[2 + m], dev), fp.at[dst, own_c], frecv.at[2 + m]))
+        for q in range(4):
+            near = pl.ds(0 if q < 2 else tile_h - 8, 8)
+            other = q ^ 1
+            out.append((corner_ok[q], remote(fcs.at[q % 2, :, near], fkr.at[other], fsend.at[6 + q], frecv.at[6 + other], corner_dev[q]), fkr.at[q], frecv.at[6 + q]))
+        return out
+
+    def place_frames():
+        for i in range(tile_h):
+            for side, base in ((0, COL_HALO - 2), (1, COL_HALO + tile_w)):
+                for m in range(2):
+                    fp[i + 2, pl.ds(base + m, 1), :] = fcr[side, m, i:i + 1, :]
+        for q in range(4):
+            base = COL_HALO - 2 if q % 2 == 0 else COL_HALO + tile_w
+            for depth in range(2):
+                i = -1 - depth if q < 2 else tile_h + depth
+                j = depth if q < 2 else 7 - depth
+                for m in range(2):
+                    fp[i + 2, pl.ds(base + m, 1), :] = fkr[q, m, j:j + 1, :]
 
     def chunk_sends(k, slot):
-        to_left = cs.at[slot, k, 0]
-        to_right = cs.at[slot, k, 1]
-        out = [(has_left, remote(to_left, cr.at[slot, 1, k], csend.at[slot, 0, k], crecv.at[slot, 1, k], left_dev)),
-               (has_right, remote(to_right, cr.at[slot, 0, k], csend.at[slot, 1, k], crecv.at[slot, 0, k], right_dev))]
+        to_left = cs.at[slot, 0, k]
+        to_right = cs.at[slot, 1, k]
+        out = [(has_left, remote(to_left, cr.at[slot, 1, k], csend.at[slot, 0], crecv.at[slot, 1, k], left_dev)),
+               (has_right, remote(to_right, cr.at[slot, 0, k], csend.at[slot, 1], crecv.at[slot, 0, k], right_dev))]
         for edge, q in ((0, 0), (n_chunks - 1, 2)):
             if k == edge:
                 out.append((corner_ok[q], remote(to_left, kr.at[slot, q + 1], ksend.at[slot, q], krecv.at[slot, q + 1], corner_dev[q])))
@@ -152,11 +162,13 @@
                 copy.start()
 
     def wait_chunk_sends(slot, cond):
-        for k in range(n_chunks):
-            for ok, copy in chunk_sends(k, slot):
-                @pl.when(both(ok, cond))
-                def _(copy=copy):
-                    copy.wait_send()
+        copies = [(ok, remote(cs.at[slot, m], cr.at[slot, m], csend.at[slot, m], csend.at[slot, m], dev))
+                  for m, (ok, dev) in enumerate(((has_left, left_dev), (has_right, right_dev)))]
+        copies += chunk_sends(0, slot)[2:] + chunk_sends(n_chunks - 1, slot)[2:]
+        for ok, copy in copies:
+            @pl.when(both(ok, cond))
+            def _(copy=copy):
+                copy.wait_send()
 
     def wait_row_send(k, slot):
         ok, copy = row_send(k, slot)
@@ -168,7 +180,7 @@
     def wait_if(ok, dst, sem, src):
         @pl.when(ok)
         def _():
-            remote(src, dst, csend.at[0, 0, 0], sem, right_dev).wait_recv()
+            remote(src, dst, csend.at[0, 0], sem, right_dev).wait_recv()
 
     sub48 = lax.broadcasted_iota(jnp.int32, (tile_w, ch), 0)
     sub16 = lax.broadcasted_iota(jnp.int32, (16, ch), 0)
@@ -181,14 +193,14 @@
         hb[slot, 0, i + 2] = pltpu.roll(v, 1, 0).astype(BF16)
         hb[slot, 2, i + 2] = pltpu.roll(v, tile_w - 1, 0).astype(BF16)
         j = i - starts[k]
-        for side, m, x in ((0, 0, 0), (0, 1, 1), (1, 0, tile_w - 2), (1, 1, tile_w - 1)):
-            cs[slot, k, side, pl.ds(8 * m + j, 1), :] = v[x:x + 1]
+        for side, m, x in edge_cells:
+            cs[slot, side, k, pl.ds(8 * m + j, 1), :] = v[x:x + 1]
         cb[2, pl.ds(i + 8, 1), :] = v[0:1]
         cb[3, pl.ds(i + 8, 1), :] = v[tile_w - 1:tile_w]
 
     def wait_cols(slot, k):
-        wait_if(has_left, cr.at[slot, 0, k], crecv.at[slot, 0, k], cs.at[slot, k, 0])
-        wait_if(has_right, cr.at[slot, 1, k], crecv.at[slot, 1, k], cs.at[slot, k, 0])
+        wait_if(has_left, cr.at[slot, 0, k], crecv.at[slot, 0, k], cs.at[slot, 0, k])
+        wait_if(has_right, cr.at[slot, 1, k], crecv.at[slot, 1, k], cs.at[slot, 0, k])
 
     def place_cols(slot, k):
         i0, n = n_ranges[k]
@@ -226,60 +238,80 @@
 
     wide = tile_w + 2 * COL_HALO
 
-    def build_x(t, slot, k):
+    def build_x(t, k):
         i0, n = r_ranges[k]
         for j in range(n):
-            parts = [pltpu.roll(fp[i0 + j + a + 1].astype(F32), lax.rem(cin * a - cin * t + cin * steps, cin * steps), 1) for a in range(3)]
+            parts = [pltpu.roll(fp[i0 + j + a + 1], lax.rem(cin * a - cin * t + cin * steps, cin * steps), 1) for a in range(3)]
             af[pl.ds(j * wide, wide)] = jnp.where(lane < cin, parts[0], jnp.where(lane < 2 * cin, parts[1], parts[2]))
         for j in range(n):
             base = j * wide + COL_HALO
             left = af[pl.ds(base - 1, tile_w)]
             mid = pltpu.roll(af[pl.ds(base, tile_w)], 64, 1)
-            xp[slot, i0 + j + 1, :, 0:LANES] = jnp.where(lane < 64, left, mid).astype(BF16)
-            xp[slot, i0 + j + 1, :, LANES:2 * LANES] = af[pl.ds(base + 1, tile_w)].astype(BF16)
+            xp[i0 + j + 1, :, 0:LANES] = jnp.where(lane < 64, left, mid).astype(BF16)
+            xp[i0 + j + 1, :, LANES:2 * LANES] = af[pl.ds(base + 1, tile_w)].astype(BF16)
         lo_half, hi_half = [], []
         for x in (-1, tile_w):
             three = [af[pl.ds(COL_HALO + x + c - 1, 8, wide)] for c in range(3)]
             lo_half.append(jnp.where(lane < 64, three[0], pltpu.roll(three[1], 64, 1)))
             hi_half.append(three[2])
-        xe[slot, k, :, 0:LANES] = jnp.concatenate(lo_half, axis=0).astype(BF16)
-        xe[slot, k, :, LANES:2 * LANES] = jnp.concatenate(hi_half, axis=0).astype(BF16)
-
-    def conv(src, i0, n, off, weights, xslot, gate, extra=None, e_lo=0):
+        xe[k, :, 0:LANES] = jnp.concatenate(lo_half, axis=0).astype(BF16)
+        xe[k, :, LANES:2 * LANES] = jnp.concatenate(hi_half, axis=0).astype(BF16)
+
+    all_taps = ["x"] + [(a, c) for c in (1, 0, 2) for a in range(3)]
+
+    def conv(src, i0, n, off, weights, gate, extra=None, e_lo=0, taps=all_taps, acc=None):
         lo, w_lo = gate * ch, (0 if gate == 2 else gate * ch)
-        acc = None
-        for c in (1, 0, 2):
-            for a in range(3):
+        for tap in taps:
+            if tap == "x":
+                lhs = xp[pl.ds(i0 + 1, n)].reshape(n * tile_w, ch)
+                more = None if extra is None else xe[extra]
+                weight = wx[:, lo:lo + ch]
+            else:
+                a, c = tap
                 lhs = src(c, pl.ds(i0 + a - 1 - off, n)).reshape(n * tile_w, ch)
-                if extra is not None:
-                    ends = [cb[3 * side + c, pl.ds(e_lo + a - 1 + 8, 8), :] for side in range(2)]
-                    lhs = jnp.concatenate([lhs, jnp.concatenate(ends, axis=0).astype(BF16)], axis=0)
-                part = jnp.dot(lhs, weights[a, c, :, w_lo:w_lo + ch], preferred_element_type=F32)
-                acc = part if acc is None else acc + part
-        lhs = xp[xslot, pl.ds(i0 + 1, n)].reshape(n * tile_w, ch)
-        if extra is not None:
-            lhs = jnp.concatenate([lhs, xe[xslot, extra]], axis=0)
-        acc = acc + jnp.dot(lhs, wx[:, lo:lo + ch], preferred_element_type=F32)
-        return acc + bv[lo:lo + ch].reshape(1, ch)
-
-    for copy in loads:
-        copy.wait()
+                more = None if extra is None else jnp.concatenate(
+                    [cb[3 * side + c, pl.ds(e_lo + a - 1 + 8, 8), :] for side in range(2)], axis=0).astype(BF16)
+                weight = weights[a, c, :, w_lo:w_lo + ch]
+            if more is not None:
+                lhs = jnp.concatenate([lhs, more], axis=0)
+            part = jnp.dot(lhs, weight, preferred_element_type=F32)
+            acc = part if acc is None else acc + part
+        return acc
+
+    def biased(acc, gate):
+        return acc + bv[gate * ch:(gate + 1) * ch].reshape(1, ch)
+
+    for k in range(n_chunks):
+        loads[k].wait()
     for k in range(n_chunks):
         i0, n = n_ranges[k]
         for i in range(i0, i0 + n):
-            publish(0, i, h32[i], k)
+            v = hraw[phys(i)]
+            h32[i] = v
+            publish(0, i, v, k)
+    for copy in frame_loads:
+        copy.wait()
+    pl.semaphore_wait(barrier, count)
+    for k in range(n_chunks):
         start_sends(k, 0, True)
-    for m, (ok, copy) in enumerate(f_descs):
-        src, dst = f_copies[m][1], f_copies[f_recv_index[m]][2]
-
-        @pl.when(ok)
-        def _(copy=copy, m=m, src=src, dst=dst):
+    pack_frames()
+    f_descs = frame_copies()
+    for ok, copy, _, _ in f_descs:
+        @pl.when(ok)
+        def _(copy=copy):
+            copy.start()
+    for ok, copy, _, _ in f_descs:
+        @pl.when(ok)
+        def _(copy=copy):
             copy.wait_send()
-            remote(src, dst, fsend.at[m], frecv.at[m], right_dev).wait_recv()
-    for k in range(n_chunks):
-        build_x(0, 0, k)
     for copy in weight_loads:
         copy.wait()
+    for ok, copy, dst, sem in f_descs:
+        @pl.when(ok)
+        def _(dst=dst, sem=sem):
+            remote(dst, dst, fsend.at[0], sem, right_dev).wait_recv()
+    place_frames()
+    build_x(0, 0)
 
     def halves(i0, n):
         return (i0, n - n // 2), (i0 + n - n // 2, n // 2)
@@ -311,14 +343,23 @@
         new = 1 - now
         wait_chunk_sends(new, t >= 1)
 
-    def stretch(t, now, k):
+    def ahead(now, k):
+        out = []
+        for h, (i0, n) in enumerate(halves(*n_ranges[k])):
+            skip = 0 if k == 0 and h == 0 else 2 if k == n_chunks - 1 and h == 1 else None
+            taps = [tap for tap in all_taps if tap == "x" or tap[0] != skip and (tap[1] == 1 or k > 0 and tap[0] < 2)][:AHEAD]
+            acc = conv(lambda c, rows: hb[now, c, rows], i0, n, -2, wzr, 0, taps=taps)
+            out.append((taps, acc))
+        return out
+
+    def stretch(t, now, k, begun, carry_on):
         new = 1 - now
         meet(t, now, k)
         r_lo, r_n = r_ranges[k]
         parts = halves(r_lo, r_n)
-        accs = [conv(lambda c, rows: hb[now, c, rows], i0, n, -2, wzr, now, 1, extra=k if h == 1 else None, e_lo=r_lo) for h, (i0, n) in enumerate(parts)]
-        gates = [sigmoid(acc) for acc in accs]
-        ends = gates[1][parts[1][1] * tile_w:]
+        accs = [conv(lambda c, rows: hb[now, c, rows], i0, n, -2, wzr, 1, extra=k if h == k % 2 else None, e_lo=r_lo) for h, (i0, n) in enumerate(parts)]
+        gates = [sigmoid(biased(acc, 1)) for acc in accs]
+        ends = gates[k % 2][parts[k % 2][1] * tile_w:]
         ends_l = ends[0:8] * cb[1, pl.ds(r_lo + 8, 8), :]
         ends_r = ends[8:16] * cb[4, pl.ds(r_lo + 8, 8), :]
         for (i0, n), gate in zip(parts, gates):
@@ -331,13 +372,20 @@
                 rb[0, i + 1] = jnp.where(sub48 == 0, ends_l[e:e + 1], pltpu.roll(v, 1, 0)).astype(BF16)
                 rb[2, i + 1] = jnp.where(sub48 == tile_w - 1, ends_r[e:e + 1], pltpu.roll(v, tile_w - 1, 0)).astype(BF16)
         parts = halves(*n_ranges[k])
-        accs = [conv(lambda c, rows: hb[now, c, rows], i0, n, -2, wzr, now, 0) for i0, n in parts]
+        for h, (i0, n) in enumerate(parts):
+            done, acc = begun[h] if begun is not None else ([], None)
+            acc = conv(lambda c, rows: hb[now, c, rows], i0, n, -2, wzr, 0, taps=[tap for tap in all_taps if tap not in done], acc=acc)
+            zb[pl.ds((i0 - n_ranges[k][0]) * tile_w, n * tile_w)] = sigmoid(biased(acc, 0))
+        if k + 1 < n_chunks:
+            build_x(t, k + 1)
+        else:
+            build_x(jnp.minimum(t + 1, steps - 1), 0)
+        accs = [conv(lambda c, rows: rb[c, rows], i0, n, -1, wn, 2) for i0, n in parts]
+        begun = None
+        if carry_on and k + 1 < n_chunks:
+            begun = ahead(now, k + 1)
         for (i0, n), acc in zip(parts, accs):
-            zb[pl.ds((i0 - n_ranges[k][0]) * tile_w, n * tile_w)] = sigmoid(acc)
-        build_x(jnp.minimum(t + 1, steps - 1), new, k)
-        accs = [conv(lambda c, rows: rb[c, rows], i0, n, -1, wn, now, 2) for i0, n in parts]
-        for (i0, n), acc in zip(parts, accs):
-            cand = jnp.tanh(acc)
+            cand = jnp.tanh(biased(acc, 2))
             for j in range(n):
                 i = i0 + j
                 mix = cand[j * tile_w:(j + 1) * tile_w]
@@ -345,11 +393,16 @@
                 h32[i] = v
                 h_seq[t, 0, phys(i)] = v.astype(BF16)
                 publish(new, i, v, k)
+        if carry_on and k + 1 == n_chunks:
+            begun = ahead(new, 0)
+        return begun
 
     def body(p, carry):
+        begun = None
         for s in range(UNROLL):
             for k in range(n_chunks):
-                stretch(UNROLL * p + s, s % 2, k)
+                last = s == UNROLL - 1 and k == n_chunks - 1
+                begun = stretch(UNROLL * p + s, s % 2, k, begun, not last)
         return carry
 
     lax.fori_loop(0, steps // UNROLL, body, 0)
@@ -371,16 +424,18 @@
         dma = pltpu.SemaphoreType.DMA
         kk = len(CHUNKS)
         wide = tile_w + 2 * COL_HALO
+        pair = (2, 2)
         scratch = [
             vm((3, 3, ch, 2 * ch), BF16), vm((3, 3, ch, ch), BF16), vm((256, 3 * ch), BF16), vm((3 * ch,), F32),
-            vm((tile_h, steps, cin, tile_w), BF16), vm((tile_h + 4, wide, LANES), BF16),
+            vm((steps, tile_h, cin, tile_w), BF16), vm((tile_h + 4, wide, LANES), F32),
+            vm(pair + (tile_h, LANES), F32), vm(pair + (tile_h, LANES), F32), vm((4, 2, 8, LANES), F32),
             vm((2, 3, tile_h + 4, tile_w, ch), BF16), vm((3, tile_h + 2, tile_w, ch), BF16),
-            vm((2, tile_h + 2, tile_w, ch), BF16), vm((2, kk, 16, ch), BF16), vm((8 * wide, LANES), F32),
-            vm((tile_h, tile_w, ch), F32), vm((max(CHUNKS) * tile_w, ch), F32),
-            vm((2, 2, tile_w, ch), F32), vm((2, 2, tile_w, ch), F32),
-            vm((2, kk, 2, 16, ch), F32), vm((2, 2, kk, 16, ch), F32), vm((2, 4, 16, ch), F32), vm((6, 48, ch), F32),
-            dma((3, tile_h)), dma((14,)), dma((14,)), dma((2, 2, kk)), dma((2, 2, kk)), dma((2, 4)), dma((2, 4)),
-            dma((2,)), dma((2, 2)),
+            vm((tile_h + 2, tile_w, ch), BF16), vm((kk, 16, ch), BF16), vm((8 * wide, LANES), F32),
+            vm((tile_h, tile_w, ch), F32), vm((tile_h, tile_w, ch), F32), vm((max(CHUNKS) * tile_w, ch), F32),
+            vm(pair + (tile_w, ch), F32), vm(pair + (tile_w, ch), F32),
+            vm(pair + (kk, 16, ch), F32), vm(pair + (kk, 16, ch), F32), vm((2, 4, 16, ch), F32), vm((6, 48, ch), F32),
+            dma((3, tile_h)), dma((10,)), dma((10,)), dma(pair), dma(pair + (kk,)), dma((2, 4)), dma((2, 4)),
+            dma((2,)), dma(pair),
         ]
 
         def body(*refs):

time: 64.6 us -> 59.9 us (0.927)
  Pallas kernels: 60.6 us -> 55.9 us
    pallas_call x1, Pallas kernels: 60.6 us -> 55.9 us  [local_fn(): pl.pallas_call(body, out_shape=(vm((steps, 1, tile_h, tile_w, ch), BF16),...]
where the time goes in v4:
time: 59.9 us; the launch traced here: 59.7 us
  Pallas kernels  55.9 us (93%)
  local copies, waits for them, and re-layouts  3.2 us (5%)
  between operations  0.64 us (1%)
    pallas_call x1, Pallas kernels, local_fn(): pl.pallas_call(body, out_shape=(vm((steps, 1, tile_h, tile_w, ch), BF16),...  55.9 us
    unnamed x2, local copies, waits for them, and re-layouts  3.2 us

profile of v4, /device:TPU:0, one launch (start us, length us, event | category | flops | bytes accessed | tf_op | source)
XLA Modules:
  0.0 59.7 jit_solution(12503448890372949221)
XLA Ops:
  0.6 55.9 %convgru.1 = (bf16[8,1,24,48,256]{4,3,2,1,0:T(8,128)(2,1)S(1)}, f32[1,24,48,256]{3,2,1,0:T(8,128)S(1)}) custom-call(bf16[8,1,24,16,48]{4,3,2,1,0:T(8,128)(2,1)} %bitcast.1, f32[1,24,48,256]{3,2,1,0:T(8,128)} %refs_1_.1, bf16[3,3,16,768]{3,2,1,0:T(8,128)(2,1)} %refs_2_.1, bf16[3,3,256,512]{3,2,1,0:T(8,128)(2,1)} %refs_3_.1, bf16[3,3,256,256]{3,2,1,0:T(8,128)(2,1)} %refs_4_.1, ...), custom_call_target="tpu_custom_call" | custom-call | tf_op jit(solution)/shard_map/convgru/pallas_call | solution.py:444
  56.5 2.2 %copy.10 = bf16[8,1,24,48,256]{4,3,2,1,0:T(8,128)(2,1)} copy(bf16[8,1,24,48,256]{4,3,2,1,0:T(8,128)(2,1)S(1)} %get-tuple-element.2) | data formatting | bytes 9437184
  58.7 1.0 %copy.11 = f32[1,24,48,256]{3,2,1,0:T(8,128)} copy(f32[1,24,48,256]{3,2,1,0:T(8,128)S(1)} %get-tuple-element.3) | data formatting | bytes 2359296

commit v5 on v4

--- a/solution.py
+++ b/solution.py
@@ -12,7 +12,8 @@
 COL_HALO = 8
 CHUNKS = (6,) * 4
 UNROLL = 2
-AHEAD = 5
+AHEAD = 4
+PART = 4
 VMEM_LIMIT = 40 * 1024 * 1024
 NAMES = ("batch", "cols", "rows")
 
@@ -57,6 +58,8 @@
         hi = tile_h + 1 if k == n_chunks - 1 else starts[k] + CHUNKS[k] + 1
         r_ranges.append((lo, hi - lo))
 
+    sides = ((has_left, left_dev), (has_right, right_dev))
+
     def remote(src, dst, s_sem, r_sem, dev):
         return pltpu.make_async_remote_copy(src_ref=src, dst_ref=dst, send_sem=s_sem, recv_sem=r_sem, device_id=dev, device_id_type=MESH)
 
@@ -75,7 +78,7 @@
             dst = wx.at[pl.ds(pl.multiple_of(64 * c + cin * la, cin), cin)]
             weight_loads.append(pltpu.make_async_copy(w_x.at[a, c], dst, load_sem.at[2, 6 + 3 * a + c]))
     weight_loads.append(pltpu.make_async_copy(bias, bv, load_sem.at[2, 15]))
-    for copy in loads + frame_loads + weight_loads:
+    for copy in frame_loads + loads + weight_loads:
         copy.start()
 
     hf[...] = jnp.zeros_like(hf)
@@ -136,15 +139,23 @@
                 for m in range(2):
                     fp[i + 2, pl.ds(base + m, 1), :] = fkr[q, m, j:j + 1, :]
 
+    def chunk_parts(k):
+        return range(pl.cdiv(CHUNKS[k], PART))
+
     def chunk_sends(k, slot):
-        to_left = cs.at[slot, 0, k]
-        to_right = cs.at[slot, 1, k]
-        out = [(has_left, remote(to_left, cr.at[slot, 1, k], csend.at[slot, 0], crecv.at[slot, 1, k], left_dev)),
-               (has_right, remote(to_right, cr.at[slot, 0, k], csend.at[slot, 1], crecv.at[slot, 0, k], right_dev))]
-        for edge, q in ((0, 0), (n_chunks - 1, 2)):
-            if k == edge:
-                out.append((corner_ok[q], remote(to_left, kr.at[slot, q + 1], ksend.at[slot, q], krecv.at[slot, q + 1], corner_dev[q])))
-                out.append((corner_ok[q + 1], remote(to_right, kr.at[slot, q], ksend.at[slot, q + 1], krecv.at[slot, q], corner_dev[q + 1])))
+        out = []
+        for p in chunk_parts(k):
+            for m, (ok, dev) in enumerate(sides):
+                out.append((ok, remote(cs.at[slot, m, k, p], cr.at[slot, 1 - m, k, p], csend.at[slot, m], crecv.at[slot, 1 - m, k, p], dev)))
+        return out
+
+    def corner_sends(k, slot):
+        out = []
+        for edge, q, p in ((0, 0, 0), (n_chunks - 1, 2, (CHUNKS[-1] - 1) // PART)):
+            for m in range(2):
+                if k == edge:
+                    to = q + 1 - m
+                    out.append((corner_ok[q + m], remote(cs.at[slot, m, k, p], kr.at[slot, to], ksend.at[slot, q + m], krecv.at[slot, to], corner_dev[q + m])))
         return out
 
     def row_send(k, slot):
@@ -153,7 +164,7 @@
         return has_last, remote(h32.at[pl.ds(tile_h - 2, 2)], hl.at[slot], vsend.at[1], vrecv.at[slot, 1], last_dev)
 
     def start_sends(k, slot, more):
-        copies = chunk_sends(k, slot)
+        copies = chunk_sends(k, slot) + corner_sends(k, slot)
         if k in (0, n_chunks - 1):
             copies.append(row_send(k, slot))
         for ok, copy in copies:
@@ -163,8 +174,8 @@
 
     def wait_chunk_sends(slot, cond):
         copies = [(ok, remote(cs.at[slot, m], cr.at[slot, m], csend.at[slot, m], csend.at[slot, m], dev))
-                  for m, (ok, dev) in enumerate(((has_left, left_dev), (has_right, right_dev)))]
-        copies += chunk_sends(0, slot)[2:] + chunk_sends(n_chunks - 1, slot)[2:]
+                  for m, (ok, dev) in enumerate(sides)]
+        copies += corner_sends(0, slot) + corner_sends(n_chunks - 1, slot)
         for ok, copy in copies:
             @pl.when(both(ok, cond))
             def _(copy=copy):
@@ -194,19 +205,21 @@
         hb[slot, 2, i + 2] = pltpu.roll(v, tile_w - 1, 0).astype(BF16)
         j = i - starts[k]
         for side, m, x in edge_cells:
-            cs[slot, side, k, pl.ds(8 * m + j, 1), :] = v[x:x + 1]
+            cs[slot, side, k, j // PART, pl.ds(PART * m + j % PART, 1), :] = v[x:x + 1]
         cb[2, pl.ds(i + 8, 1), :] = v[0:1]
         cb[3, pl.ds(i + 8, 1), :] = v[tile_w - 1:tile_w]
 
-    def wait_cols(slot, k):
-        wait_if(has_left, cr.at[slot, 0, k], crecv.at[slot, 0, k], cs.at[slot, 0, k])
-        wait_if(has_right, cr.at[slot, 1, k], crecv.at[slot, 1, k], cs.at[slot, 0, k])
-
-    def place_cols(slot, k):
+    def wait_cols(slot, k, p):
+        for m, (ok, _) in enumerate(sides):
+            wait_if(ok, cr.at[slot, m, k, p], crecv.at[slot, m, k, p], cs.at[slot, 0, k, p])
+
+    def place_cols(slot, k, p):
         i0, n = n_ranges[k]
+        n = min(n - p * PART, PART)
+        i0 = i0 + p * PART
         for side in range(2):
             for m in range(2):
-                cb[4 * side + m, pl.ds(i0 + 8, n), :] = cr[slot, side, k, 8 * m:8 * m + n, :]
+                cb[4 * side + m, pl.ds(i0 + 8, n), :] = cr[slot, side, k, p, PART * m:PART * m + n, :]
         for i in range(i0, i0 + n):
             old = hb[slot, 0, i + 2, 0:16].astype(F32)
             hb[slot, 0, i + 2, 0:16] = jnp.where(sub16 == 0, row_of(1, i), old).astype(BF16)
@@ -218,17 +231,17 @@
         wait_if(ok, src.at[slot], vrecv.at[slot, last], h32.at[pl.ds(0, 2)])
         for m in range(2):
             q = 2 * last + m
-            wait_if(corner_ok[q], kr.at[slot, q], krecv.at[slot, q], cs.at[slot, 0, 0])
+            wait_if(corner_ok[q], kr.at[slot, q], krecv.at[slot, q], cs.at[slot, 0, 0, 0])
 
     def place_rows(slot, last):
         src = hl if last else hf
         for depth in range(2):
             i = tile_h + depth if last else -1 - depth
             m = 1 - depth if last else depth
-            j = CHUNKS[-1] - 1 - depth if last else depth
+            j = (CHUNKS[-1] - 1 - depth if last else depth) % PART
             for x in range(2):
-                cb[x, pl.ds(i + 8, 1), :] = kr[slot, 2 * last, 8 * x + j:8 * x + j + 1, :]
-                cb[4 + x, pl.ds(i + 8, 1), :] = kr[slot, 2 * last + 1, 8 * x + j:8 * x + j + 1, :]
+                cb[x, pl.ds(i + 8, 1), :] = kr[slot, 2 * last, PART * x + j:PART * x + j + 1, :]
+                cb[4 + x, pl.ds(i + 8, 1), :] = kr[slot, 2 * last + 1, PART * x + j:PART * x + j + 1, :]
             v = src[slot, m]
             cb[2, pl.ds(i + 8, 1), :] = v[0:1]
             cb[3, pl.ds(i + 8, 1), :] = v[tile_w - 1:tile_w]
@@ -281,6 +294,15 @@
     def biased(acc, gate):
         return acc + bv[gate * ch:(gate + 1) * ch].reshape(1, ch)
 
+    for copy in frame_loads:
+        copy.wait()
+    pack_frames()
+    f_descs = frame_copies()
+    pl.semaphore_wait(barrier, count)
+    for ok, copy, _, _ in f_descs:
+        @pl.when(ok)
+        def _(copy=copy):
+            copy.start()
     for k in range(n_chunks):
         loads[k].wait()
     for k in range(n_chunks):
@@ -289,17 +311,8 @@
             v = hraw[phys(i)]
             h32[i] = v
             publish(0, i, v, k)
-    for copy in frame_loads:
-        copy.wait()
-    pl.semaphore_wait(barrier, count)
     for k in range(n_chunks):
         start_sends(k, 0, True)
-    pack_frames()
-    f_descs = frame_copies()
-    for ok, copy, _, _ in f_descs:
-        @pl.when(ok)
-        def _(copy=copy):
-            copy.start()
     for ok, copy, _, _ in f_descs:
         @pl.when(ok)
         def _(copy=copy):
@@ -321,22 +334,23 @@
         if k == 0:
             start_sends(n_chunks - 1, now, both(t > 0, True))
             free_slot(t, now)
-            wait_cols(now, 0)
             wait_rows(now, 0)
             wait_row_send(0, now)
         else:
             start_sends(k - 1, new, t < steps - 1)
+        fresh = [(k, p) for p in chunk_parts(k) if p or not k]
         if k + 1 < n_chunks:
-            wait_cols(now, k + 1)
+            fresh.append((k + 1, 0))
         else:
             wait_rows(now, 1)
             wait_row_send(n_chunks - 1, now)
+        for item in fresh:
+            wait_cols(now, *item)
+        for item in fresh:
+            place_cols(now, *item)
         if k == 0:
-            place_cols(now, 0)
             place_rows(now, 0)
-        if k + 1 < n_chunks:
-            place_cols(now, k + 1)
-        else:
+        if k + 1 == n_chunks:
             place_rows(now, 1)
 
     def free_slot(t, now):
@@ -347,7 +361,7 @@
         out = []
         for h, (i0, n) in enumerate(halves(*n_ranges[k])):
             skip = 0 if k == 0 and h == 0 else 2 if k == n_chunks - 1 and h == 1 else None
-            taps = [tap for tap in all_taps if tap == "x" or tap[0] != skip and (tap[1] == 1 or k > 0 and tap[0] < 2)][:AHEAD]
+            taps = [tap for tap in all_taps[:AHEAD] if tap == "x" or tap[0] != skip]
             acc = conv(lambda c, rows: hb[now, c, rows], i0, n, -2, wzr, 0, taps=taps)
             out.append((taps, acc))
         return out
@@ -433,8 +447,8 @@
             vm((tile_h + 2, tile_w, ch), BF16), vm((kk, 16, ch), BF16), vm((8 * wide, LANES), F32),
             vm((tile_h, tile_w, ch), F32), vm((tile_h, tile_w, ch), F32), vm((max(CHUNKS) * tile_w, ch), F32),
             vm(pair + (tile_w, ch), F32), vm(pair + (tile_w, ch), F32),
-            vm(pair + (kk, 16, ch), F32), vm(pair + (kk, 16, ch), F32), vm((2, 4, 16, ch), F32), vm((6, 48, ch), F32),
-            dma((3, tile_h)), dma((10,)), dma((10,)), dma(pair), dma(pair + (kk,)), dma((2, 4)), dma((2, 4)),
+            vm(pair + (kk, 2, 8, ch), F32), vm(pair + (kk, 2, 8, ch), F32), vm((2, 4, 8, ch), F32), vm((6, 48, ch), F32),
+            dma((3, tile_h)), dma((10,)), dma((10,)), dma(pair), dma(pair + (kk, 2)), dma((2, 4)), dma((2, 4)),
             dma((2,)), dma(pair),
         ]
 

time: 59.9 us -> 59.2 us (0.988)
  Pallas kernels: 55.9 us -> 55.2 us
    pallas_call x1, Pallas kernels: 55.9 us -> 55.2 us  [local_fn(): pl.pallas_call(body, out_shape=(vm((steps, 1, tile_h, tile_w, ch), BF16),...]
where the time goes in v5:
time: 59.2 us; the launch traced here: 59 us
  Pallas kernels  55.2 us (93%)
  local copies, waits for them, and re-layouts  3.2 us (5%)
  between operations  0.64 us (1%)
    pallas_call x1, Pallas kernels, local_fn(): pl.pallas_call(body, out_shape=(vm((steps, 1, tile_h, tile_w, ch), BF16),...  55.2 us
    unnamed x2, local copies, waits for them, and re-layouts  3.2 us

profile of v5, /device:TPU:0, one launch (start us, length us, event | category | flops | bytes accessed | tf_op | source)
XLA Modules:
  0.0 59.0 jit_solution(15241229967690196908)
XLA Ops:
  0.6 55.2 %convgru.1 = (bf16[8,1,24,48,256]{4,3,2,1,0:T(8,128)(2,1)S(1)}, f32[1,24,48,256]{3,2,1,0:T(8,128)S(1)}) custom-call(bf16[8,1,24,16,48]{4,3,2,1,0:T(8,128)(2,1)} %bitcast.1, f32[1,24,48,256]{3,2,1,0:T(8,128)} %refs_1_.1, bf16[3,3,16,768]{3,2,1,0:T(8,128)(2,1)} %refs_2_.1, bf16[3,3,256,512]{3,2,1,0:T(8,128)(2,1)} %refs_3_.1, bf16[3,3,256,256]{3,2,1,0:T(8,128)(2,1)} %refs_4_.1, ...), custom_call_target="tpu_custom_call" | custom-call | tf_op jit(solution)/shard_map/convgru/pallas_call | solution.py:458
  55.8 2.2 %copy.10 = bf16[8,1,24,48,256]{4,3,2,1,0:T(8,128)(2,1)} copy(bf16[8,1,24,48,256]{4,3,2,1,0:T(8,128)(2,1)S(1)} %get-tuple-element.2) | data formatting | bytes 9437184
  58.0 1.0 %copy.11 = f32[1,24,48,256]{3,2,1,0:T(8,128)} copy(f32[1,24,48,256]{3,2,1,0:T(8,128)S(1)} %get-tuple-element.3) | data formatting | bytes 2359296

commit v6 on v5

--- a/solution.py
+++ b/solution.py
@@ -303,16 +303,17 @@
         @pl.when(ok)
         def _(copy=copy):
             copy.start()
-    for k in range(n_chunks):
-        loads[k].wait()
-    for k in range(n_chunks):
-        i0, n = n_ranges[k]
-        for i in range(i0, i0 + n):
-            v = hraw[phys(i)]
-            h32[i] = v
-            publish(0, i, v, k)
-    for k in range(n_chunks):
-        start_sends(k, 0, True)
+    for group in ((0, 1), range(2, n_chunks)):
+        for k in group:
+            loads[k].wait()
+        for k in group:
+            i0, n = n_ranges[k]
+            for i in range(i0, i0 + n):
+                v = hraw[phys(i)]
+                h32[i] = v
+                publish(0, i, v, k)
+        for k in group:
+            start_sends(k, 0, True)
     for ok, copy, _, _ in f_descs:
         @pl.when(ok)
         def _(copy=copy):
@@ -455,7 +456,7 @@
         def body(*refs):
             kernel_body(n_cols, n_rows, dims, *refs)
 
-        return pl.pallas_call(
+        results = pl.pallas_call(
             body,
             out_shape=(vm((steps, 1, tile_h, tile_w, ch), BF16), vm((1, tile_h, tile_w, ch), F32)),
             in_specs=[pl.BlockSpec(memory_space=pltpu.HBM)] * 6,
@@ -465,4 +466,21 @@
             name="convgru",
         )(*[pltpu.with_memory_space_constraint(v, pltpu.HBM) for v in (jnp.swapaxes(frames, 3, 4), h_init, w_x, w_hzr, w_hn, gate_bias)])
 
+        def drain(seq_in, last_in, seq_out, last_out, sems):
+            copies = [pltpu.make_async_copy(src, dst, sems.at[m]) for m, (src, dst) in enumerate(((seq_in, seq_out), (last_in, last_out)))]
+            for copy in copies:
+                copy.start()
+            for copy in copies:
+                copy.wait()
+
+        return pl.pallas_call(
+            drain,
+            out_shape=[jax.ShapeDtypeStruct(v.shape, v.dtype) for v in results],
+            in_specs=[pl.BlockSpec(memory_space=vm)] * 2,
+            out_specs=[pl.BlockSpec(memory_space=pltpu.HBM)] * 2,
+            scratch_shapes=[dma((2,))],
+            compiler_params=pltpu.CompilerParams(vmem_limit_bytes=VMEM_LIMIT // 8),
+            name="drain",
+        )(*[pltpu.with_memory_space_constraint(v, vm) for v in results])
+
     return jax.shard_map(local_fn, mesh=mesh, in_specs=(frame_spec, state_spec, P(), P(), P(), P()), out_specs=(frame_spec, state_spec), check_vma=False)

time: 59.2 us -> 58.6 us (0.990)
  local copies, waits for them, and re-layouts: 3.2 us -> 0 us
  Pallas kernels: 55.2 us -> 57.8 us
    unnamed x2 -> x0, local copies, waits for them, and re-layouts: 3.2 us -> none
    pallas_call x0 -> x1, Pallas kernels: none -> 2.59 us  [local_fn(): pl.pallas_call(drain, out_shape=[jax.ShapeDtypeStruct(v.shape, v.dtype) f...]
where the time goes in v6:
time: 58.6 us; the launch traced here: 58.4 us
  Pallas kernels  57.8 us (99%)
  between operations  0.64 us (1%)
    pallas_call x1, Pallas kernels, local_fn(): pl.pallas_call(body, out_shape=(vm((steps, 1, tile_h, tile_w, ch), BF16),...  55.2 us
    pallas_call x1, Pallas kernels, local_fn(): pl.pallas_call(drain, out_shape=[jax.ShapeDtypeStruct(v.shape, v.dtype) f...  2.59 us

profile of v6, /device:TPU:0, one launch (start us, length us, event | category | flops | bytes accessed | tf_op | source)
XLA Modules:
  0.0 58.4 jit_solution(2298507948980136876)
XLA Ops:
  0.6 55.2 %convgru.1 = (bf16[8,1,24,48,256]{4,3,2,1,0:T(8,128)(2,1)S(1)}, f32[1,24,48,256]{3,2,1,0:T(8,128)S(1)}) custom-call(bf16[8,1,24,16,48]{4,3,2,1,0:T(8,128)(2,1)} %bitcast.1, f32[1,24,48,256]{3,2,1,0:T(8,128)} %refs_1_.1, bf16[3,3,16,768]{3,2,1,0:T(8,128)(2,1)} %refs_2_.1, bf16[3,3,256,512]{3,2,1,0:T(8,128)(2,1)} %refs_3_.1, bf16[3,3,256,256]{3,2,1,0:T(8,128)(2,1)} %refs_4_.1, ...), custom_call_target="tpu_custom_call" | custom-call | tf_op jit(solution)/shard_map/convgru/pallas_call | solution.py:459
  55.8 2.6 %drain.1 = (bf16[8,1,24,48,256]{4,3,2,1,0:T(8,128)(2,1)}, f32[1,24,48,256]{3,2,1,0:T(8,128)}) custom-call(bf16[8,1,24,48,256]{4,3,2,1,0:T(8,128)(2,1)S(1)} %get-tuple-element.4.seq_in, f32[1,24,48,256]{3,2,1,0:T(8,128)S(1)} %get-tuple-element.5.last_in), custom_call_target="tpu_custom_call" | custom-call | tf_op jit(solution)/shard_map/drain/pallas_call | solution.py:476

commit v7 on v6

--- a/solution.py
+++ b/solution.py
@@ -13,7 +13,7 @@
 CHUNKS = (6,) * 4
 UNROLL = 2
 AHEAD = 4
-PART = 4
+PART = 2
 VMEM_LIMIT = 40 * 1024 * 1024
 NAMES = ("batch", "cols", "rows")
 
@@ -448,8 +448,8 @@
             vm((tile_h + 2, tile_w, ch), BF16), vm((kk, 16, ch), BF16), vm((8 * wide, LANES), F32),
             vm((tile_h, tile_w, ch), F32), vm((tile_h, tile_w, ch), F32), vm((max(CHUNKS) * tile_w, ch), F32),
             vm(pair + (tile_w, ch), F32), vm(pair + (tile_w, ch), F32),
-            vm(pair + (kk, 2, 8, ch), F32), vm(pair + (kk, 2, 8, ch), F32), vm((2, 4, 8, ch), F32), vm((6, 48, ch), F32),
-            dma((3, tile_h)), dma((10,)), dma((10,)), dma(pair), dma(pair + (kk, 2)), dma((2, 4)), dma((2, 4)),
+            vm(pair + (kk, 3, 2 * PART, ch), F32), vm(pair + (kk, 3, 2 * PART, ch), F32), vm((2, 4, 2 * PART, ch), F32), vm((6, 48, ch), F32),
+            dma((3, tile_h)), dma((10,)), dma((10,)), dma(pair), dma(pair + (kk, 3)), dma((2, 4)), dma((2, 4)),
             dma((2,)), dma(pair),
         ]
 

time: 58.6 us -> 59.1 us (level)
  no operation moved by 1% of the time
where the time goes in v7:
time: 59.1 us; the launch traced here: 58.9 us
  Pallas kernels  58.3 us (99%)
  between operations  0.64 us (1%)
    pallas_call x1, Pallas kernels, local_fn(): pl.pallas_call(body, out_shape=(vm((steps, 1, tile_h, tile_w, ch), BF16),...  55.7 us
    pallas_call x1, Pallas kernels, local_fn(): pl.pallas_call(drain, out_shape=[jax.ShapeDtypeStruct(v.shape, v.dtype) f...  2.59 us

profile of v7, /device:TPU:0, one launch (start us, length us, event | category | flops | bytes accessed | tf_op | source)
XLA Modules:
  0.0 58.9 jit_solution(13853606807188318094)
XLA Ops:
  0.6 55.7 %convgru.1 = (bf16[8,1,24,48,256]{4,3,2,1,0:T(8,128)(2,1)S(1)}, f32[1,24,48,256]{3,2,1,0:T(8,128)S(1)}) custom-call(bf16[8,1,24,16,48]{4,3,2,1,0:T(8,128)(2,1)} %bitcast.1, f32[1,24,48,256]{3,2,1,0:T(8,128)} %refs_1_.1, bf16[3,3,16,768]{3,2,1,0:T(8,128)(2,1)} %refs_2_.1, bf16[3,3,256,512]{3,2,1,0:T(8,128)(2,1)} %refs_3_.1, bf16[3,3,256,256]{3,2,1,0:T(8,128)(2,1)} %refs_4_.1, ...), custom_call_target="tpu_custom_call" | custom-call | tf_op jit(solution)/shard_map/convgru/pallas_call | solution.py:459
  56.3 2.6 %drain.1 = (bf16[8,1,24,48,256]{4,3,2,1,0:T(8,128)(2,1)}, f32[1,24,48,256]{3,2,1,0:T(8,128)}) custom-call(bf16[8,1,24,48,256]{4,3,2,1,0:T(8,128)(2,1)S(1)} %get-tuple-element.4.seq_in, f32[1,24,48,256]{3,2,1,0:T(8,128)S(1)} %get-tuple-element.5.last_in), custom_call_target="tpu_custom_call" | custom-call | tf_op jit(solution)/shard_map/drain/pallas_call | solution.py:476
